TPU v7x, 32 devices: a whole 2x2x4 slice. The times are simulated.
32 devices in a mesh: mol: 2 (over x), pts: 16 (over z, y, core).
Axes of the slice: x: 2, y: 2, z: 4, core: 2. Of those that a mesh axis runs over, the one named last changes fastest.
Arguments:
- points_map: bfloat16 [12800, 800], P(('mol', 'pts')), parts along dimension 0, may hold values from -0.21875 to 0.21875
- trial: bfloat16 [12800, 128], P('mol'), parts along dimension 0, may hold values from -6 to 6
- core: bfloat16 [12800, 6400], P(('mol', 'pts')), parts along dimension 0, may hold values from -2 to 4, as said below
- walkers: bfloat16 [1600, 12, 128], P('mol'), parts along dimension 0, may hold values from -6 to 6
- draws: int32 [12800, 12], P(('mol', 'pts')), parts along dimension 0, may hold values from 0 to 3
Outputs:
- new_walkers: bfloat16 [1600, 12, 128], P(('mol', 'pts')), parts along dimension 0
- energy: float32 [24], P('mol'), parts along dimension 0
There are 2 independent parts, one for each index of `mol`. A program takes and returns all parts, laid end to end along the dimension named above; each array names one. Nothing has to cross between parts.
Inputs may be any that keep to these rules, and one draw needn't show every extreme that they name: core is symmetric.
All inputs are finite; a program needn't handle non-finite values.
Results may differ from a plain program's by a relative error of at most 0.018.
Values may be sent and summed in bfloat16 or wider, within the bound.
A program may use at most 192 MiB of HBM per device.

v0:
```python
import functools
import math

import jax
import jax.numpy as jnp
from jax import lax
from jax.experimental import pallas as pl
from jax.experimental.pallas import tpu as pltpu
from jax.sharding import PartitionSpec as P

TAYLOR = 3


GAUSS_NODES = (-2.3344142, -0.7419637, 0.7419637, 2.3344142)
FIELD_STEP = 0.15
LANES = 128
CONTRACT_LAST = (((1,), (1,)), ((), ()))
CONTRACT_FIRST = (((0,), (0,)), ((), ()))


def node_lookup(draws):
    values = jnp.zeros(draws.shape, jnp.float32)
    for number, node in enumerate(GAUSS_NODES):
        values = values + jnp.where(draws == number, node, 0.0).astype(jnp.float32)
    return values


def dot(left, right, dims):
    return lax.dot_general(left, right, dims, preferred_element_type=jnp.float32)


def add_exchange(out_ref, blocks, map_block, trial_ref, trial_own, core_ref, walkers_ref, orbit_own, first, weight):
    rows, occupied = trial_own.shape
    window = blocks.shape[0]
    base = pl.multiple_of(first // LANES * LANES, LANES)
    shift = pl.multiple_of(first - base, 16)
    blocks[...] = jnp.zeros_like(blocks)
    blocks[pl.ds(shift, rows), :] = dot(map_block, walkers_ref[...], (((1,), (0,)), ((), ()))).astype(jnp.bfloat16)
    core_here = core_ref[:, pl.ds(base, window)].astype(jnp.float32)
    trial_there = trial_ref[pl.ds(base, window), :]
    for walker in range(out_ref.shape[0]):
        cols = slice(walker * occupied, (walker + 1) * occupied)
        forward = dot(orbit_own[:, cols], trial_there, CONTRACT_LAST)
        backward = dot(trial_own[...], blocks[:, cols], CONTRACT_LAST)
        product = core_here * forward * backward
        out_ref[walker] += weight * jnp.sum(product.reshape(rows // 8, 8, window), axis=0)


def spread_field(field_ref, here, piece, start, own, occupied):
    walker_ids = (start + lax.broadcasted_iota(jnp.int32, (1, own), 1)) // occupied
    low = start // occupied
    field = field_ref[here, :]
    lane = lax.broadcasted_iota(jnp.int32, field.shape, 1)
    spread = jnp.zeros((piece, own), jnp.float32)
    for offset in range((own + occupied - 2) // occupied + 1):
        column = jnp.sum(jnp.where(lane == low + offset, field, 0.0), axis=1, keepdims=True)
        spread = jnp.where(walker_ids == low + offset, column, spread)
    return spread


def fused_kernel(
    n, piece, own_map, trial_ref, trial_own, core_ref, walkers_ref, orbit_own, field_ref, cols_ref,
    sums_ref, out_ref,
    blocks, gathered, wide, total, term, right_sems, left_sems, side_sems, recv_sems,
):
    rows, occupied = trial_own.shape
    own = cols_ref.shape[0]
    points = gathered.shape[0]
    chips = n // 2
    far = chips // 2
    top = (rows // 2 + 15) // 16 * 16
    parts = ((0, top), (top, rows - top))
    me = lax.axis_index("pts")
    core_id = lax.rem(me, 2)
    chip = me // 2
    ring = jnp.where(lax.rem(chip, 2) == 0, chip // 2, chips - 1 - chip // 2)

    def device(place, side):
        place = lax.rem(place + 2 * chips, chips)
        where = jnp.where(place < far, 2 * place, 2 * (chips - 1 - place) + 1)
        return 2 * where + side

    right, left, partner = device(ring + 1, core_id), device(ring - 1, core_id), device(ring, 1 - core_id)

    def slot(index, part=None):
        offset, length = (0, rows) if part is None else parts[part]
        return gathered.at[pl.ds(pl.multiple_of(index * rows + offset, 16), length), :]

    def send(src, index, part, send_sem, target):
        return pltpu.make_async_remote_copy(
            src_ref=src,
            dst_ref=slot(index, part),
            send_sem=send_sem,
            recv_sem=recv_sems.at[index, part or 0],
            device_id={"pts": target},
            device_id_type=pl.DeviceIdType.MESH,
        )

    def forward(index, part, send_sem, target):
        send(slot(index, part), index, part, send_sem, target).start()

    def arrived(index, part=None):
        send(slot(index, part), index, part, side_sems.at[0, 0], partner).wait_recv()

    barrier = pltpu.get_barrier_semaphore()
    for other in (right, left, partner):
        pl.semaphore_signal(barrier, inc=1, device_id={"pts": other}, device_id_type=pl.DeviceIdType.MESH)
    pl.semaphore_wait(barrier, 3)
    send(own_map, me, None, right_sems.at[0], right).start()
    send(own_map, me, None, left_sems.at[0], left).start()
    send(own_map, me, None, side_sems.at[0, 0], partner).start()
    gathered[pl.ds(pl.multiple_of(me * rows, 16), rows), :] = own_map[...]
    sums_ref[...] = jnp.zeros_like(sums_ref)
    total[...] = jnp.zeros_like(total)
    term[...] = cols_ref[...]

    def add_block(index):
        here = pl.ds(pl.multiple_of(index * rows, 16), rows)
        block = gathered[here, :]
        spread = spread_field(field_ref, here, rows, me * own, own, occupied)
        wide[here, :] = spread
        current = dot(block, term[...], CONTRACT_LAST).astype(jnp.bfloat16)
        scaled = (spread * current.astype(jnp.float32)).astype(jnp.bfloat16)
        total[...] += dot(scaled, block, CONTRACT_FIRST)

    @pl.loop(0, 2 * far + 1)
    def _(task):
        hop = task // 2
        same = lax.rem(task, 2) == 0
        ahead, behind = device(ring + hop, core_id), device(ring - hop, core_id)
        ahead_side, behind_side = device(ring + hop, 1 - core_id), device(ring - hop, 1 - core_id)
        last = hop == far
        middle = jnp.logical_and(hop > 0, hop < far)

        @pl.when(jnp.logical_and(same, middle))
        def _():
            arrived(behind)

            @pl.when(hop < far - 1)
            def _():
                forward(behind, None, right_sems.at[hop], right)

            @pl.when(hop == far - 1)
            def _():
                forward(behind, 0, right_sems.at[hop], right)

            forward(behind, None, side_sems.at[0, hop], partner)
            arrived(ahead)

            @pl.when(hop < far - 1)
            def _():
                forward(ahead, None, left_sems.at[hop], left)

            @pl.when(hop == far - 1)
            def _():
                forward(ahead, 1, left_sems.at[hop], left)

            forward(ahead, None, side_sems.at[1, hop], partner)

        @pl.when(last)
        def _():
            for part in range(2):
                arrived(ahead, part)
                forward(ahead, part, side_sems.at[part, hop], partner)
            for part in range(2):
                arrived(ahead_side, part)

        @pl.when(jnp.logical_not(same))
        def _():
            arrived(ahead_side)

            @pl.when(hop > 0)
            def _():
                arrived(behind_side)

        near = jnp.where(same, ahead, ahead_side)
        opposite = jnp.where(last, ahead_side, jnp.where(same, behind, behind_side))
        pair = jnp.where(jnp.logical_and(last, ring >= far), ahead_side, near)
        add_exchange(
            sums_ref, blocks, gathered[pl.ds(pl.multiple_of(pair * rows, 16), rows), :], trial_ref, trial_own,
            core_ref, walkers_ref, orbit_own, pair * rows, jnp.where(hop == 0, 1.0, 2.0),
        )
        add_block(near)

        @pl.when(hop > 0)
        def _():
            add_block(opposite)

    running = cols_ref[...].astype(jnp.float32)
    for degree in range(1, TAYLOR + 1):
        if degree > 1:
            total[...] = jnp.zeros_like(total)

            @pl.loop(0, points // piece)
            def _(number):
                here = pl.ds(pl.multiple_of(number * piece, piece), piece)
                block = gathered[here, :]
                current = dot(block, term[...], CONTRACT_LAST).astype(jnp.bfloat16)
                scaled = (wide[here, :] * current.astype(jnp.float32)).astype(jnp.bfloat16)
                total[...] += dot(scaled, block, CONTRACT_FIRST)

        term[...] = (total[...] / degree).astype(jnp.bfloat16)
        running = running + term[...].astype(jnp.float32)
    out_ref[...] = running.astype(jnp.bfloat16)

    for hop in range(far):
        for number, (sems, target) in enumerate(((right_sems, right), (left_sems, left))):
            part = number if hop == far - 1 and hop > 0 else None
            send(slot(me, part), me, part, sems.at[hop], target).wait_send()
    send(slot(me), me, None, side_sems.at[0, 0], partner).wait_send()
    for hop in range(1, far + 1):
        for number in range(2):
            part = number if hop == far else None
            send(slot(me, part), me, part, side_sems.at[number, hop], partner).wait_send()


def fused(n, points_map, trial, trial_here, core, flat_walkers, orbit, field_full, own_cols_t, walker_count):
    rows, orbitals = points_map.shape
    points, own, columns = rows * n, own_cols_t.shape[0], flat_walkers.shape[1]
    window = (rows + (LANES - 16) + LANES - 1) // LANES * LANES
    far = n // 4
    piece = next(p for p in (1280, 640, 256, rows) if points % p == 0)
    dma = pltpu.SemaphoreType.DMA
    return pl.pallas_call(
        functools.partial(fused_kernel, n, piece),
        out_shape=(
            jax.ShapeDtypeStruct((walker_count, 8, window), jnp.float32),
            jax.ShapeDtypeStruct((own, orbitals), jnp.bfloat16),
        ),
        in_specs=[pl.BlockSpec(memory_space=pltpu.VMEM)] * 8,
        out_specs=[pl.BlockSpec(memory_space=pltpu.VMEM)] * 2,
        scratch_shapes=[
            pltpu.VMEM((window, columns), jnp.bfloat16),
            pltpu.VMEM((points, orbitals), jnp.bfloat16),
            pltpu.VMEM((points, own), jnp.float32),
            pltpu.VMEM((own, orbitals), jnp.float32),
            pltpu.VMEM((own, orbitals), jnp.bfloat16),
            dma((far,)),
            dma((far,)),
            dma((2, far + 1)),
            dma((n, 2)),
        ],
        compiler_params=pltpu.CompilerParams(
            collective_id=0, has_side_effects=True, vmem_limit_bytes=60 * 2**20
        ),
        name="fused",
    )(points_map, trial, trial_here, core, flat_walkers, orbit, field_full, own_cols_t)


def propagate_kernel(n, occupied, piece, map_ref, field_ref, cols_ref, out_ref, wide, total, term):
    points, orbitals = map_ref.shape
    own = cols_ref.shape[0]
    start = lax.axis_index("pts") * own
    walker_ids = (start + lax.broadcasted_iota(jnp.int32, (1, own), 1)) // occupied
    low = start // occupied
    span = (own + occupied - 2) // occupied + 1
    running = cols_ref[...].astype(jnp.float32)
    term[...] = cols_ref[...]
    for degree in range(1, TAYLOR + 1):
        total[...] = jnp.zeros_like(total)

        @pl.loop(0, points // piece)
        def _(number):
            here = pl.ds(pl.multiple_of(number * piece, piece), piece)
            if degree == 1:
                field = field_ref[here, :]
                lane = lax.broadcasted_iota(jnp.int32, field.shape, 1)
                spread = jnp.zeros((piece, own), jnp.float32)
                for offset in range(span):
                    column = jnp.sum(jnp.where(lane == low + offset, field, 0.0), axis=1, keepdims=True)
                    spread = jnp.where(walker_ids == low + offset, column, spread)
                wide[here, :] = spread
            block = map_ref[here, :]
            current = dot(block, term[...], CONTRACT_LAST).astype(jnp.bfloat16)
            scaled = (wide[here, :] * current.astype(jnp.float32)).astype(jnp.bfloat16)
            total[...] += dot(scaled, block, CONTRACT_FIRST)

        term[...] = (total[...] / degree).astype(jnp.bfloat16)
        running = running + term[...].astype(jnp.float32)
    out_ref[...] = running.astype(jnp.bfloat16)


def propagate(n, occupied, map_full, field_full, own_cols_t):
    points, orbitals = map_full.shape
    own = own_cols_t.shape[0]
    piece = next(p for p in (1280, 640, 256, points // n) if points % p == 0)
    return pl.pallas_call(
        functools.partial(propagate_kernel, n, occupied, piece),
        out_shape=jax.ShapeDtypeStruct((own, orbitals), jnp.bfloat16),
        in_specs=[pl.BlockSpec(memory_space=pltpu.VMEM)] * 3,
        out_specs=pl.BlockSpec(memory_space=pltpu.VMEM),
        scratch_shapes=[
            pltpu.VMEM((points, own), jnp.float32),
            pltpu.VMEM((own, orbitals), jnp.float32),
            pltpu.VMEM((own, orbitals), jnp.bfloat16),
        ],
        cost_estimate=pl.CostEstimate(
            flops=12 * points * orbitals * own, bytes_accessed=2 * map_full.size, transcendentals=0
        ),
        compiler_params=pltpu.CompilerParams(vmem_limit_bytes=60 * 2**20),
        name="propagate",
    )(map_full, field_full, own_cols_t)


def exchange_plain(trial, trial_here, core, orbit):
    core_block = core.astype(jnp.float32)

    def per_walker(operands):
        left_orb, right_orb = operands
        forward = jnp.dot(left_orb, trial.T, preferred_element_type=jnp.float32)
        backward = jnp.dot(trial_here, right_orb.T, preferred_element_type=jnp.float32)
        return jnp.sum(core_block * forward * backward)

    everyone = lax.all_gather(orbit, "pts", axis=0, tiled=True)
    return lax.map(per_walker, (jnp.moveaxis(orbit, 1, 0), jnp.moveaxis(everyone, 1, 0)))


def gather_stacked(part):
    n = lax.axis_size("pts")
    copies = jnp.broadcast_to(part[None], (n,) + part.shape)
    return lax.all_to_all(copies, "pts", split_axis=0, concat_axis=0, tiled=True)


def body(points_map, trial, core, walkers, draws):
    point_rows = points_map.shape[0]
    orbitals = points_map.shape[1]
    walker_count = walkers.shape[1]
    occupied = walkers.shape[2]
    n = lax.axis_size("pts")
    point_first = lax.axis_index("pts") * point_rows
    trial_here = lax.dynamic_slice_in_dim(trial, point_first, point_rows, 0)
    flat_walkers = walkers.reshape(orbitals, walker_count * occupied)
    flat_orbit = jnp.dot(points_map, flat_walkers, preferred_element_type=jnp.float32).astype(jnp.bfloat16)
    orbit = flat_orbit.reshape(point_rows, walker_count, occupied)
    density = (
        jnp.sum(orbit.astype(jnp.float32) * trial_here.astype(jnp.float32)[:, None, :], axis=2)
        / math.sqrt(occupied)
    ).astype(jnp.bfloat16)
    potential = jnp.dot(
        core,
        jnp.moveaxis(gather_stacked(density.T), 2, 1).reshape(point_rows * n, walker_count),
        preferred_element_type=jnp.float32,
    )
    field = FIELD_STEP * (node_lookup(draws) - FIELD_STEP * potential)
    field_full = jnp.moveaxis(gather_stacked(field.T), 2, 1).reshape(point_rows * n, walker_count)
    own_rows = orbitals // n
    own_cols = walker_count * occupied // n
    col_start = lax.axis_index("pts") * own_cols
    cols_walkers = lax.dynamic_slice_in_dim(flat_walkers, col_start, own_cols, 1)
    if point_rows % 16 == 0 and n % 8 == 0:
        sums, final_t = fused(
            n, points_map, trial, trial_here, core, flat_walkers, flat_orbit, field_full, cols_walkers.T, walker_count
        )
        exchange = jnp.sum(sums, axis=(1, 2))
    else:
        map_full = lax.all_gather(points_map, "pts", axis=0, tiled=True)
        final_t = propagate(n, occupied, map_full, field_full, cols_walkers.T)
        exchange = exchange_plain(trial, trial_here, core, orbit)
    placed = lax.all_to_all(final_t.T, "pts", split_axis=0, concat_axis=1, tiled=True)
    hartree = jnp.sum(density.astype(jnp.float32) * potential, axis=0)
    total_points = point_rows * n
    energy = jnp.sum(gather_stacked((hartree - exchange / occupied) / (2.0 * total_points)), axis=0)
    return (placed.reshape(own_rows, walker_count, occupied), energy)


def solution(mesh):
    placed = (
        P(("mol", "pts"), None),
        P("mol", None),
        P(("mol", "pts"), None),
        P("mol", None, None),
        P(("mol", "pts"), None),
    )
    return jax.shard_map(
        body,
        mesh=mesh,
        in_specs=placed,
        out_specs=(P(("mol", "pts"), None, None), P("mol")),
        check_vma=False,
    )
```

profile of v0, /device:TPU:0, one launch (start us, length us, event | category | flops | bytes accessed | tf_op | source)
XLA Modules:
  0.0 177.8 jit_solution(11797013711300748730)
XLA Ops:
  0.6 0.0 copy-start.2
  0.6 3.3 %copy.41 = bf16[800,12,128]{0,2,1:T(8,128)(2,1)S(1)} copy(bf16[800,12,128]{2,0,1:T(8,128)(2,1)} %param.8) | data formatting | bytes 4915200 | tf_op args[3]
  3.9 0.0 copy-start
  4.0 1.5 copy-done
  5.5 0.0 copy-done.2
  5.5 2.5 %convolution_convert_fusion.orbit_own = bf16[400,1536]{1,0:T(8,128)(2,1)} fusion(bf16[400,800]{1,0:T(8,128)(2,1)S(1)} %copy-done.2, bf16[800,1536]{0,1:T(8,128)(2,1)S(1)} %bitcast.23), kind=kOutput, calls=%fused_computation.1 | convolution fusion | flops 983654400 | bytes 4326400 | tf_op jit(solution)/shard_map/dot_general | solution.py:333
  8.0 2.5 %reshape.43 = f32[400,12,128]{2,1,0:T(8,128)S(1)} reshape(bf16[400,1536]{1,0:T(8,128)(2,1)} %convolution_convert_fusion.orbit_own) | data formatting | bytes 3686400 | tf_op jit(solution)/shard_map/convert_element_type | solution.py:336
  10.5 1.6 fusion.1
  12.1 0.0 copy-start.3
  12.1 0.9 multiply_reduce_fusion
  13.0 0.1 copy.42
  13.2 17.2 %all_to_all.32 = bf16[16,12,400]{2,1,0:T(8,128)(2,1)S(1)} all-to-all(bf16[16,12,400]{2,1,0:T(8,128)(2,1)S(1)} %broadcast_in_dim.44), channel_id=1, replica_groups=mesh['mol'=2,'pts'=16] {'pts'}, dimensions={0} | all-to-all | bytes 307200 | tf_op jit(solution)/shard_map/all_to_all | solution.py:321
  30.4 0.1 copy.43
  30.5 0.3 reshape.40
  30.8 0.0 copy-done.3
  30.9 0.0 copy-start.1
  30.9 4.2 %multiply_reduce_fusion.1 = (f32[12]{0:T(128)S(1)}, f32[12,400]{1,0:T(8,128)S(1)}) fusion(f32[400,12]{0,1:T(8,128)S(1)} %copy.42, s32[400,12]{0,1:T(8,128)S(1)} %copy-done.3, bf16[6400,12]{0,1:T(8,128)(2,1)S(1)} %reshape.40, bf16[400,6400]{1,0:T(8,128)(2,1)} %core_ref.1), kind=kOutput, calls=%fused_computation.4 | convolution fusion | flops 61531188 | bytes 5331248 | tf_op jit(solution)/shard_map/dot_general | solution.py:339
  35.0 0.9 broadcast_in_dim.45
  35.9 3.8 %all-to-all-start.1 = ((f32[16,12,400]{2,1,0:T(8,128)}), f32[16,12,400]{2,1,0:T(8,128)S(1)}, u32[]{:S(2)}, u32[]{:S(2)}) async-start(f32[16,12,400]{2,1,0:T(8,128)} %broadcast_in_dim.45), calls=%async_computation.1 | async-start | bytes 1048576 | tf_op jit(solution)/shard_map/all_to_all | solution.py:321
  39.7 0.0 copy-done.1
  39.7 2.8 %copy.45.walkers_ref = bf16[800,1536]{1,0:T(8,128)(2,1)} copy(bf16[800,1536]{0,1:T(8,128)(2,1)S(1)} %bitcast.24) | data formatting | bytes 4915200 | tf_op jit(solution)/shard_map/reshape | solution.py:332
  42.5 0.7 dynamic-slice_bitcast_fusion.cols_ref
  43.2 10.6 %all-to-all-done.1 = f32[16,12,400]{2,1,0:T(8,128)S(1)} async-done(((f32[16,12,400]{2,1,0:T(8,128)}), f32[16,12,400]{2,1,0:T(8,128)S(1)}, u32[]{:S(2)}, u32[]{:S(2)}) %all-to-all-start.1) | async-done | bytes 307232 | tf_op jit(solution)/shard_map/all_to_all | solution.py:321
  53.7 2.3 %copy.44 = f32[16,400,12]{2,1,0:T(8,128)} copy(f32[16,400,12]{1,2,0:T(8,128)S(1)} %bitcast.26) | data formatting | bytes 614400 | tf_op jit(solution)/shard_map/transpose | solution.py:345
  56.0 93.3 %fused.1 = (f32[12,8,512]{2,1,0:T(8,128)}, bf16[96,800]{1,0:T(8,128)(2,1)}) custom-call(bf16[400,800]{1,0:T(8,128)(2,1)} %own_map.1, bf16[6400,128]{1,0:T(8,128)(2,1)} %trial_ref.1, bf16[400,128]{1,0:T(8,128)(2,1)} %get-tuple-element.17.trial_own, bf16[400,6400]{1,0:T(8,128)(2,1)} %core_ref.1, bf16[800,1536]{1,0:T(8,128)(2,1)} %copy.45.walkers_ref, ...), custom_call_target="tpu_custom_call" | custom-call | tf_op jit(solution)/shard_map/fused/pallas_call | solution.py:224
  149.3 1.1 reduce_sum.38
  150.4 0.6 broadcast_in_dim.46
  151.0 6.5 %all-to-all-start.3 = ((f32[16,1,12]{2,1,0:T(1,128)}), f32[16,1,12]{2,1,0:T(1,128)S(1)}, u32[]{:S(2)}, u32[]{:S(2)}) async-start(f32[16,1,12]{2,1,0:T(1,128)} %broadcast_in_dim.46), calls=%async_computation.3 | async-start | bytes 16384 | tf_op jit(solution)/shard_map/all_to_all | solution.py:321
  157.5 1.1 copy.46
  158.6 0.7 all_to_all.24
  159.3 4.5 %all-to-all-done.3 = f32[16,1,12]{2,1,0:T(1,128)S(1)} async-done(((f32[16,1,12]{2,1,0:T(1,128)}), f32[16,1,12]{2,1,0:T(1,128)S(1)}, u32[]{:S(2)}, u32[]{:S(2)}) %all-to-all-start.3) | async-done | bytes 800 | tf_op jit(solution)/shard_map/all_to_all | solution.py:321
  163.9 3.5 %all-to-all-start.2 = ((bf16[16,50,96]{2,1,0:T(8,128)(2,1)}), bf16[16,50,96]{2,1,0:T(8,128)(2,1)S(1)}, u32[]{:S(2)}, u32[]{:S(2)}) async-start(bf16[16,50,96]{2,1,0:T(8,128)(2,1)} %all_to_all.24), calls=%async_computation.2 | async-start | bytes 458752 | tf_op jit(solution)/shard_map/all_to_all | solution.py:359
  167.4 0.5 reduce_sum.39
  167.9 8.9 %all-to-all-done.2 = bf16[16,50,96]{2,1,0:T(8,128)(2,1)S(1)} async-done(((bf16[16,50,96]{2,1,0:T(8,128)(2,1)}), bf16[16,50,96]{2,1,0:T(8,128)(2,1)S(1)}, u32[]{:S(2)}, u32[]{:S(2)}) %all-to-all-start.2) | async-done | bytes 153632 | tf_op jit(solution)/shard_map/all_to_all | solution.py:359
  176.9 0.2 reshape.42
  177.1 0.7 copy.49
  (4 shorter events, 0.1 us)
Async XLA Ops:
  0.6 4.9 %copy-start.2 = (bf16[400,800]{1,0:T(8,128)(2,1)S(1)}, bf16[400,800]{1,0:T(8,128)(2,1)}, u32[]{:S(2)}) copy-start(bf16[400,800]{1,0:T(8,128)(2,1)} %own_map.1) | copy-start | bytes 1920004
  3.9 1.5 copy-start
  12.1 18.8 %copy-start.3 = (s32[400,12]{0,1:T(8,128)S(1)}, s32[400,12]{0,1:T(8,128)}, u32[]{:S(2)}) copy-start(s32[400,12]{0,1:T(8,128)} %param.9) | copy-start | bytes 57604
  30.9 8.8 %copy-start.1 = (bf16[800,12,128]{0,2,1:T(8,128)(2,1)S(1)}, bf16[800,12,128]{0,2,1:T(8,128)(2,1)}, u32[]{:S(2)}) copy-start(bf16[800,12,128]{0,2,1:T(8,128)(2,1)} %copy-done) | copy-start | bytes 7372804
  35.9 17.8 %all-to-all-start.1 = ((f32[16,12,400]{2,1,0:T(8,128)}), f32[16,12,400]{2,1,0:T(8,128)S(1)}, u32[]{:S(2)}, u32[]{:S(2)}) async-start(f32[16,12,400]{2,1,0:T(8,128)} %broadcast_in_dim.45), calls=%async_computation.1 | async-start | bytes 1048576 | tf_op jit(solution)/shard_map/all_to_all | solution.py:321
  151.0 12.8 %all-to-all-start.3 = ((f32[16,1,12]{2,1,0:T(1,128)}), f32[16,1,12]{2,1,0:T(1,128)S(1)}, u32[]{:S(2)}, u32[]{:S(2)}) async-start(f32[16,1,12]{2,1,0:T(1,128)} %broadcast_in_dim.46), calls=%async_computation.3 | async-start | bytes 16384 | tf_op jit(solution)/shard_map/all_to_all | solution.py:321
  163.9 13.0 %all-to-all-start.2 = ((bf16[16,50,96]{2,1,0:T(8,128)(2,1)}), bf16[16,50,96]{2,1,0:T(8,128)(2,1)S(1)}, u32[]{:S(2)}, u32[]{:S(2)}) async-start(bf16[16,50,96]{2,1,0:T(8,128)(2,1)} %all_to_all.24), calls=%async_computation.2 | async-start | bytes 458752 | tf_op jit(solution)/shard_map/all_to_all | solution.py:359
where the time goes:
time: 178 us
  Pallas kernels  93.3 us (52%)
  waiting for transfers between devices  24 us (13%)
  local copies, waits for them, and re-layouts  17.9 us (10%)
  blocking collectives  17.2 us (10%)
  starting transfers between devices  13.7 us (8%)
  matrix products  6.69 us (4%)
  other arithmetic  4.16 us (2%)
    pallas_call x1, Pallas kernels, fused(): pl.pallas_call(functools.partial(fused_kernel, n, piece), out_shape=(jax....  93.3 us
    all_to_all x1, blocking collectives, gather_stacked(): lax.all_to_all(copies, 'pts', split_axis=0, concat_axis=0, tiled=True)  17.2 us
    all_to_all x2, waiting for transfers between devices, gather_stacked(): lax.all_to_all(copies, 'pts', split_axis=0, concat_axis=0, tiled=True)  15.1 us
    all_to_all x2, starting transfers between devices, gather_stacked(): lax.all_to_all(copies, 'pts', split_axis=0, concat_axis=0, tiled=True)  10.2 us
    all_to_all x1, waiting for transfers between devices, body(): lax.all_to_all(final_t.T, 'pts', split_axis=0, concat_axis=1, tiled=True)  8.91 us
    unnamed x10, local copies, waits for them, and re-layouts  5.56 us
    dot_general x1, matrix products, body(): jnp.dot(core, jnp.moveaxis(gather_stacked(density.T), 2, 1).reshape(point...  4.17 us
  transfers between devices with their start and end apart: 3, of which 3 were waited for; matrix products, arithmetic and copies ran while one was open for 3% of the time, Pallas kernels for 0%

commit v1 on v0

--- a/solution.py
+++ b/solution.py
@@ -29,43 +29,20 @@
     return lax.dot_general(left, right, dims, preferred_element_type=jnp.float32)
 
 
-def add_exchange(out_ref, blocks, map_block, trial_ref, trial_own, core_ref, walkers_ref, orbit_own, first, weight):
-    rows, occupied = trial_own.shape
+def fused_kernel(
+    n, walker_count, map_hbm, trial_hbm, core_hbm, walkers_hbm, draws_ref, out_ref, energy_ref,
+    gathered, trial_ref, core_ref, walkers_ref, orbit_own, blocks, sums, total, term,
+    dens_own, dens_slots, dens_full, field_own, field_slots, fields, chosen, energy_own, energy_slots, pick, outgoing, incoming,
+    local_sems, right_sems, left_sems, side_sems, recv_sems, dens_sems, field_sems, energy_sems, out_sems,
+):
+    rows, columns = orbit_own.shape
+    occupied = trial_ref.shape[1]
+    own, orbitals = total.shape
+    points = gathered.shape[0]
     window = blocks.shape[0]
-    base = pl.multiple_of(first // LANES * LANES, LANES)
-    shift = pl.multiple_of(first - base, 16)
-    blocks[...] = jnp.zeros_like(blocks)
-    blocks[pl.ds(shift, rows), :] = dot(map_block, walkers_ref[...], (((1,), (0,)), ((), ()))).astype(jnp.bfloat16)
-    core_here = core_ref[:, pl.ds(base, window)].astype(jnp.float32)
-    trial_there = trial_ref[pl.ds(base, window), :]
-    for walker in range(out_ref.shape[0]):
-        cols = slice(walker * occupied, (walker + 1) * occupied)
-        forward = dot(orbit_own[:, cols], trial_there, CONTRACT_LAST)
-        backward = dot(trial_own[...], blocks[:, cols], CONTRACT_LAST)
-        product = core_here * forward * backward
-        out_ref[walker] += weight * jnp.sum(product.reshape(rows // 8, 8, window), axis=0)
-
-
-def spread_field(field_ref, here, piece, start, own, occupied):
-    walker_ids = (start + lax.broadcasted_iota(jnp.int32, (1, own), 1)) // occupied
-    low = start // occupied
-    field = field_ref[here, :]
-    lane = lax.broadcasted_iota(jnp.int32, field.shape, 1)
-    spread = jnp.zeros((piece, own), jnp.float32)
-    for offset in range((own + occupied - 2) // occupied + 1):
-        column = jnp.sum(jnp.where(lane == low + offset, field, 0.0), axis=1, keepdims=True)
-        spread = jnp.where(walker_ids == low + offset, column, spread)
-    return spread
-
-
-def fused_kernel(
-    n, piece, own_map, trial_ref, trial_own, core_ref, walkers_ref, orbit_own, field_ref, cols_ref,
-    sums_ref, out_ref,
-    blocks, gathered, wide, total, term, right_sems, left_sems, side_sems, recv_sems,
-):
-    rows, occupied = trial_own.shape
-    own = cols_ref.shape[0]
-    points = gathered.shape[0]
+    own_rows = out_ref.shape[0]
+    lines = dens_own.shape[0]
+    span = chosen.shape[0]
     chips = n // 2
     far = chips // 2
     top = (rows // 2 + 15) // 16 * 16
@@ -82,46 +59,127 @@
 
     right, left, partner = device(ring + 1, core_id), device(ring - 1, core_id), device(ring, 1 - core_id)
 
+    def rows_of(index):
+        return pl.ds(pl.multiple_of(index * rows, 16), rows)
+
     def slot(index, part=None):
         offset, length = (0, rows) if part is None else parts[part]
         return gathered.at[pl.ds(pl.multiple_of(index * rows + offset, 16), length), :]
 
-    def send(src, index, part, send_sem, target):
+    def remote(src, dst, send_sem, recv_sem, target):
         return pltpu.make_async_remote_copy(
             src_ref=src,
-            dst_ref=slot(index, part),
+            dst_ref=dst,
             send_sem=send_sem,
-            recv_sem=recv_sems.at[index, part or 0],
+            recv_sem=recv_sem,
             device_id={"pts": target},
             device_id_type=pl.DeviceIdType.MESH,
         )
 
+    def send(index, part, send_sem, target):
+        return remote(slot(index, part), slot(index, part), send_sem, recv_sems.at[index, part or 0], target)
+
     def forward(index, part, send_sem, target):
-        send(slot(index, part), index, part, send_sem, target).start()
+        send(index, part, send_sem, target).start()
 
     def arrived(index, part=None):
-        send(slot(index, part), index, part, side_sems.at[0, 0], partner).wait_recv()
-
+        send(index, part, side_sems.at[0, 0], partner).wait_recv()
+
+    def to_everyone(source, slots, sems):
+        for step in range(1, n):
+            peer = lax.rem(me + step, n)
+            remote(source(peer), slots.at[me], sems.at[0, step], sems.at[1, me], peer).start()
+
+    def from_everyone(source, slots, sems):
+        for step in range(1, n):
+            peer = lax.rem(me + step, n)
+            remote(source(peer), slots.at[peer], sems.at[0, step], sems.at[1, peer], peer).wait_recv()
+
+    def all_sent(source, slots, sems):
+        for step in range(1, n):
+            peer = lax.rem(me + step, n)
+            remote(source(peer), slots.at[me], sems.at[0, step], sems.at[1, me], peer).wait_send()
+
+    own_here = rows_of(me)
+    local = [
+        pltpu.make_async_copy(map_hbm, gathered.at[own_here, :], local_sems.at[0]),
+        pltpu.make_async_copy(walkers_hbm, walkers_ref, local_sems.at[1]),
+        pltpu.make_async_copy(trial_hbm, trial_ref, local_sems.at[2]),
+        pltpu.make_async_copy(core_hbm, core_ref, local_sems.at[3]),
+    ]
+    for copy in local:
+        copy.start()
     barrier = pltpu.get_barrier_semaphore()
-    for other in (right, left, partner):
-        pl.semaphore_signal(barrier, inc=1, device_id={"pts": other}, device_id_type=pl.DeviceIdType.MESH)
-    pl.semaphore_wait(barrier, 3)
-    send(own_map, me, None, right_sems.at[0], right).start()
-    send(own_map, me, None, left_sems.at[0], left).start()
-    send(own_map, me, None, side_sems.at[0, 0], partner).start()
-    gathered[pl.ds(pl.multiple_of(me * rows, 16), rows), :] = own_map[...]
-    sums_ref[...] = jnp.zeros_like(sums_ref)
+    for step in range(1, n):
+        pl.semaphore_signal(
+            barrier, inc=1, device_id={"pts": lax.rem(me + step, n)}, device_id_type=pl.DeviceIdType.MESH
+        )
+    sums[...] = jnp.zeros_like(sums)
     total[...] = jnp.zeros_like(total)
-    term[...] = cols_ref[...]
-
-    def add_block(index):
-        here = pl.ds(pl.multiple_of(index * rows, 16), rows)
-        block = gathered[here, :]
-        spread = spread_field(field_ref, here, rows, me * own, own, occupied)
-        wide[here, :] = spread
-        current = dot(block, term[...], CONTRACT_LAST).astype(jnp.bfloat16)
-        scaled = (spread * current.astype(jnp.float32)).astype(jnp.bfloat16)
-        total[...] += dot(scaled, block, CONTRACT_FIRST)
+    local[0].wait()
+    pl.semaphore_wait(barrier, n - 1)
+    send(me, None, right_sems.at[0], right).start()
+    send(me, None, left_sems.at[0], left).start()
+    send(me, None, side_sems.at[0, 0], partner).start()
+
+    local[1].wait()
+    local[2].wait()
+    orbit_own[...] = dot(gathered[own_here, :], walkers_ref[...], (((1,), (0,)), ((), ()))).astype(jnp.bfloat16)
+    trial_own = trial_ref[own_here, :].astype(jnp.float32)
+    lane = lax.broadcasted_iota(jnp.int32, (rows, LANES), 1)
+    density = jnp.zeros((rows, LANES), jnp.float32)
+    for walker in range(walker_count):
+        cols = slice(walker * occupied, (walker + 1) * occupied)
+        column = jnp.sum(orbit_own[:, cols].astype(jnp.float32) * trial_own, axis=1, keepdims=True)
+        density = jnp.where(lane == walker, column, density)
+    density = (density / math.sqrt(occupied)).astype(jnp.bfloat16)
+    unit = (
+        lax.broadcasted_iota(jnp.int32, (lines, LANES), 0) == lax.broadcasted_iota(jnp.int32, (lines, LANES), 1)
+    ).astype(jnp.bfloat16)
+    density_t = dot(unit, density, CONTRACT_LAST)
+
+    def placed(index):
+        return pl.multiple_of(index * rows // LANES * LANES, LANES), lax.rem(index * rows, LANES)
+
+    base, shift = placed(me)
+    field_own[...] = jnp.zeros_like(field_own)
+    field_own[:, :rows] = density_t
+    shifted = pltpu.roll(field_own[...], shift, 1).astype(jnp.bfloat16)
+    dens_own[...] = shifted
+    dens_slots[me] = shifted
+    to_everyone(lambda peer: dens_own, dens_slots, dens_sems)
+
+    start = me * own
+    left_col = pl.multiple_of(jnp.minimum(start // LANES * LANES, columns - 2 * LANES), LANES)
+    choose = (
+        lax.broadcasted_iota(jnp.int32, (own, 2 * LANES), 0) + (start - left_col)
+        == lax.broadcasted_iota(jnp.int32, (own, 2 * LANES), 1)
+    ).astype(jnp.bfloat16)
+    cols_own = dot(choose, walkers_ref[:, pl.ds(left_col, 2 * LANES)], CONTRACT_LAST).astype(jnp.bfloat16)
+    term[...] = cols_own
+    running = cols_own.astype(jnp.float32)
+    out_line = lax.broadcasted_iota(jnp.int32, pick.shape, 0)
+    out_row = lax.rem(out_line, outgoing.shape[1])
+    wanted = jnp.where(out_row < own_rows, out_line // outgoing.shape[1] * own_rows + out_row, -1)
+    pick[...] = (wanted == lax.broadcasted_iota(jnp.int32, pick.shape, 1)).astype(jnp.bfloat16)
+    local[3].wait()
+
+    def exchange(pair, weight):
+        first = pair * rows
+        block_base, block_shift = placed(pair)
+        block_shift = pl.multiple_of(block_shift, 16)
+        blocks[...] = jnp.zeros_like(blocks)
+        blocks[pl.ds(block_shift, rows), :] = dot(
+            gathered[rows_of(pair), :], walkers_ref[...], (((1,), (0,)), ((), ()))
+        ).astype(jnp.bfloat16)
+        core_here = core_ref[:, pl.ds(block_base, window)].astype(jnp.float32)
+        trial_there = trial_ref[pl.ds(block_base, window), :]
+        for walker in range(walker_count):
+            cols = slice(walker * occupied, (walker + 1) * occupied)
+            ahead_dot = dot(orbit_own[:, cols], trial_there, CONTRACT_LAST)
+            back_dot = dot(trial_ref[own_here, :], blocks[:, cols], CONTRACT_LAST)
+            product = core_here * ahead_dot * back_dot
+            sums[walker] += weight * jnp.sum(product.reshape(rows // 8, 8, window), axis=0)
 
     @pl.loop(0, 2 * far + 1)
     def _(task):
@@ -174,77 +232,158 @@
                 arrived(behind_side)
 
         near = jnp.where(same, ahead, ahead_side)
-        opposite = jnp.where(last, ahead_side, jnp.where(same, behind, behind_side))
         pair = jnp.where(jnp.logical_and(last, ring >= far), ahead_side, near)
-        add_exchange(
-            sums_ref, blocks, gathered[pl.ds(pl.multiple_of(pair * rows, 16), rows), :], trial_ref, trial_own,
-            core_ref, walkers_ref, orbit_own, pair * rows, jnp.where(hop == 0, 1.0, 2.0),
-        )
-        add_block(near)
-
-        @pl.when(hop > 0)
+        exchange(pair, jnp.where(hop == 0, 1.0, 2.0))
+
+        @pl.when(task == 1)
         def _():
-            add_block(opposite)
-
-    running = cols_ref[...].astype(jnp.float32)
+            from_everyone(lambda peer: dens_own, dens_slots, dens_sems)
+            dens_full[...] = jnp.zeros_like(dens_full)
+            for index in range(n):
+                there = pl.ds(index * rows // LANES * LANES, window)
+                dens_full[:, there] += dens_slots[index].astype(jnp.float32)
+            potential = dot(dens_full[...].astype(jnp.bfloat16), core_ref[...], CONTRACT_LAST)[:walker_count]
+            field = FIELD_STEP * (node_lookup(draws_ref[...]) - FIELD_STEP * potential)
+            hartree = jnp.sum(density_t[:walker_count] * potential, axis=1, keepdims=True)
+            energy_own[...] = jnp.zeros_like(energy_own)
+            energy_own[:walker_count, :] = jnp.broadcast_to(hartree, (walker_count, LANES))
+            field_own[...] = jnp.zeros_like(field_own)
+            field_own[:walker_count, :rows] = field
+            turned = pltpu.roll(field_own[...], shift, 1)
+            for line in range(walker_count):
+                fields[line] = turned[line : line + 1]
+            to_everyone(lambda peer: fields.at[pl.ds(peer * own // occupied, span)], field_slots, field_sems)
+            field_slots[me] = fields[pl.ds(start // occupied, span)]
+
+    walker_exchange = jnp.sum(jnp.sum(sums[...], axis=1), axis=1, keepdims=True)
+    energy_own[:walker_count, :] = (energy_own[:walker_count, :] - walker_exchange / occupied) / (2.0 * points)
+    energy_slots[me] = energy_own[...]
+    to_everyone(lambda peer: energy_own, energy_slots, energy_sems)
+    from_everyone(lambda peer: fields.at[pl.ds(peer * own // occupied, span)], field_slots, field_sems)
+    chosen[...] = jnp.zeros_like(chosen)
+    for index in range(n):
+        there = pl.ds(index * rows // LANES * LANES, window)
+        for line in range(span):
+            chosen[line, :, there] += field_slots[index, line]
+
+    piece = next(p for p in (1280, 640, 256, points) if points % p == 0)
+    owner = (start + lax.broadcasted_iota(jnp.int32, (own, 1), 0)) // occupied - start // occupied
     for degree in range(1, TAYLOR + 1):
         if degree > 1:
             total[...] = jnp.zeros_like(total)
 
-            @pl.loop(0, points // piece)
-            def _(number):
-                here = pl.ds(pl.multiple_of(number * piece, piece), piece)
-                block = gathered[here, :]
-                current = dot(block, term[...], CONTRACT_LAST).astype(jnp.bfloat16)
-                scaled = (wide[here, :] * current.astype(jnp.float32)).astype(jnp.bfloat16)
-                total[...] += dot(scaled, block, CONTRACT_FIRST)
+        @pl.loop(0, points // piece)
+        def _(number):
+            here = pl.ds(pl.multiple_of(number * piece, piece), piece)
+            block = gathered[here, :]
+            current = dot(term[...], block, CONTRACT_LAST).astype(jnp.bfloat16).astype(jnp.float32)
+            spread = chosen[0, :, here]
+            for line in range(1, span):
+                spread = jnp.where(owner == line, chosen[line, :, here], spread)
+            scaled = (spread * current).astype(jnp.bfloat16)
+            total[...] += dot(scaled, block, (((1,), (0,)), ((), ())))
 
         term[...] = (total[...] / degree).astype(jnp.bfloat16)
         running = running + term[...].astype(jnp.float32)
-    out_ref[...] = running.astype(jnp.bfloat16)
-
+
+    picked = dot(pick[...], running.astype(jnp.bfloat16), CONTRACT_LAST)
+    height = outgoing.shape[1]
+    for index in range(n):
+        outgoing[index, :, :own] = picked[index * height : (index + 1) * height].astype(jnp.bfloat16)
+    to_everyone(lambda peer: outgoing.at[peer], incoming, out_sems)
+    incoming[me] = outgoing[me]
+    from_everyone(lambda peer: energy_own, energy_slots, energy_sems)
+    energy = energy_slots[0]
+    for index in range(1, n):
+        energy = energy + energy_slots[index]
+    energy_ref[...] = energy
+    from_everyone(lambda peer: outgoing.at[peer], incoming, out_sems)
+    out_lane = lax.broadcasted_iota(jnp.int32, (height, LANES), 1)
+    for number in range(columns // LANES):
+        tile = jnp.zeros((height, LANES), jnp.float32)
+        for index in range(n):
+            offset = index * own - number * LANES
+            if -own < offset < LANES:
+                moved = incoming[index].astype(jnp.float32)
+                if offset % LANES:
+                    moved = pltpu.roll(moved, offset % LANES, 1)
+                keep = jnp.logical_and(out_lane >= offset, out_lane < offset + own)
+                tile = jnp.where(keep, moved, tile)
+        out_ref[:, number * LANES : (number + 1) * LANES] = tile[:own_rows].astype(jnp.bfloat16)
+
+    all_sent(lambda peer: dens_own, dens_slots, dens_sems)
+    all_sent(lambda peer: fields.at[pl.ds(peer * own // occupied, span)], field_slots, field_sems)
+    all_sent(lambda peer: energy_own, energy_slots, energy_sems)
+    all_sent(lambda peer: outgoing.at[peer], incoming, out_sems)
     for hop in range(far):
         for number, (sems, target) in enumerate(((right_sems, right), (left_sems, left))):
             part = number if hop == far - 1 and hop > 0 else None
-            send(slot(me, part), me, part, sems.at[hop], target).wait_send()
-    send(slot(me), me, None, side_sems.at[0, 0], partner).wait_send()
+            send(me, part, sems.at[hop], target).wait_send()
+    send(me, None, side_sems.at[0, 0], partner).wait_send()
     for hop in range(1, far + 1):
         for number in range(2):
             part = number if hop == far else None
-            send(slot(me, part), me, part, side_sems.at[number, hop], partner).wait_send()
-
-
-def fused(n, points_map, trial, trial_here, core, flat_walkers, orbit, field_full, own_cols_t, walker_count):
+            send(me, part, side_sems.at[number, hop], partner).wait_send()
+
+
+def fused(n, points_map, trial, core, flat_walkers, draws_t, walker_count):
     rows, orbitals = points_map.shape
-    points, own, columns = rows * n, own_cols_t.shape[0], flat_walkers.shape[1]
+    points, occupied = trial.shape
+    columns = flat_walkers.shape[1]
+    own, own_rows = columns // n, orbitals // n
+    lines = (walker_count + 1 + 15) // 16 * 16
+    span = (own + occupied - 2) // occupied + 1
+    height = (own_rows + 15) // 16 * 16
     window = (rows + (LANES - 16) + LANES - 1) // LANES * LANES
+    full = (points - rows) // LANES * LANES + window
     far = n // 4
-    piece = next(p for p in (1280, 640, 256, rows) if points % p == 0)
     dma = pltpu.SemaphoreType.DMA
+    vmem = pltpu.VMEM
     return pl.pallas_call(
-        functools.partial(fused_kernel, n, piece),
+        functools.partial(fused_kernel, n, walker_count),
         out_shape=(
-            jax.ShapeDtypeStruct((walker_count, 8, window), jnp.float32),
-            jax.ShapeDtypeStruct((own, orbitals), jnp.bfloat16),
+            jax.ShapeDtypeStruct((own_rows, columns), jnp.bfloat16),
+            jax.ShapeDtypeStruct((lines, LANES), jnp.float32),
         ),
-        in_specs=[pl.BlockSpec(memory_space=pltpu.VMEM)] * 8,
+        in_specs=[pl.BlockSpec(memory_space=pl.ANY)] * 4 + [pl.BlockSpec(memory_space=pltpu.VMEM)],
         out_specs=[pl.BlockSpec(memory_space=pltpu.VMEM)] * 2,
         scratch_shapes=[
-            pltpu.VMEM((window, columns), jnp.bfloat16),
-            pltpu.VMEM((points, orbitals), jnp.bfloat16),
-            pltpu.VMEM((points, own), jnp.float32),
-            pltpu.VMEM((own, orbitals), jnp.float32),
-            pltpu.VMEM((own, orbitals), jnp.bfloat16),
+            vmem((points, orbitals), jnp.bfloat16),
+            vmem((points, occupied), jnp.bfloat16),
+            vmem((rows, points), jnp.bfloat16),
+            vmem((orbitals, columns), jnp.bfloat16),
+            vmem((rows, columns), jnp.bfloat16),
+            vmem((window, columns), jnp.bfloat16),
+            vmem((walker_count, 8, window), jnp.float32),
+            vmem((own, orbitals), jnp.float32),
+            vmem((own, orbitals), jnp.bfloat16),
+            vmem((lines, window), jnp.bfloat16),
+            vmem((n, lines, window), jnp.bfloat16),
+            vmem((lines, full), jnp.float32),
+            vmem((lines, window), jnp.float32),
+            vmem((n, span, 1, window), jnp.float32),
+            vmem((lines, 1, window), jnp.float32),
+            vmem((span, 1, full), jnp.float32),
+            vmem((lines, LANES), jnp.float32),
+            vmem((n, lines, LANES), jnp.float32),
+            vmem((n * height, orbitals), jnp.bfloat16),
+            vmem((n, height, LANES), jnp.bfloat16),
+            vmem((n, height, LANES), jnp.bfloat16),
+            dma((4,)),
             dma((far,)),
             dma((far,)),
             dma((2, far + 1)),
             dma((n, 2)),
+            dma((2, n)),
+            dma((2, n)),
+            dma((2, n)),
+            dma((2, n)),
         ],
         compiler_params=pltpu.CompilerParams(
             collective_id=0, has_side_effects=True, vmem_limit_bytes=60 * 2**20
         ),
         name="fused",
-    )(points_map, trial, trial_here, core, flat_walkers, orbit, field_full, own_cols_t)
+    )(points_map, trial, core, flat_walkers, draws_t)
 
 
 def propagate_kernel(n, occupied, piece, map_ref, field_ref, cols_ref, out_ref, wide, total, term):
@@ -327,9 +466,14 @@
     walker_count = walkers.shape[1]
     occupied = walkers.shape[2]
     n = lax.axis_size("pts")
+    own_rows = orbitals // n
+    own_cols = walker_count * occupied // n
+    flat_walkers = walkers.reshape(orbitals, walker_count * occupied)
+    if point_rows % 16 == 0 and n % 8 == 0 and own_cols <= LANES and occupied == LANES:
+        placed, energy = fused(n, points_map, trial, core, flat_walkers, draws.T, walker_count)
+        return placed.reshape(own_rows, walker_count, occupied), energy[:walker_count, 0]
     point_first = lax.axis_index("pts") * point_rows
     trial_here = lax.dynamic_slice_in_dim(trial, point_first, point_rows, 0)
-    flat_walkers = walkers.reshape(orbitals, walker_count * occupied)
     flat_orbit = jnp.dot(points_map, flat_walkers, preferred_element_type=jnp.float32).astype(jnp.bfloat16)
     orbit = flat_orbit.reshape(point_rows, walker_count, occupied)
     density = (
@@ -343,19 +487,11 @@
     )
     field = FIELD_STEP * (node_lookup(draws) - FIELD_STEP * potential)
     field_full = jnp.moveaxis(gather_stacked(field.T), 2, 1).reshape(point_rows * n, walker_count)
-    own_rows = orbitals // n
-    own_cols = walker_count * occupied // n
     col_start = lax.axis_index("pts") * own_cols
     cols_walkers = lax.dynamic_slice_in_dim(flat_walkers, col_start, own_cols, 1)
-    if point_rows % 16 == 0 and n % 8 == 0:
-        sums, final_t = fused(
-            n, points_map, trial, trial_here, core, flat_walkers, flat_orbit, field_full, cols_walkers.T, walker_count
-        )
-        exchange = jnp.sum(sums, axis=(1, 2))
-    else:
-        map_full = lax.all_gather(points_map, "pts", axis=0, tiled=True)
-        final_t = propagate(n, occupied, map_full, field_full, cols_walkers.T)
-        exchange = exchange_plain(trial, trial_here, core, orbit)
+    map_full = lax.all_gather(points_map, "pts", axis=0, tiled=True)
+    final_t = propagate(n, occupied, map_full, field_full, cols_walkers.T)
+    exchange = exchange_plain(trial, trial_here, core, orbit)
     placed = lax.all_to_all(final_t.T, "pts", split_axis=0, concat_axis=1, tiled=True)
     hartree = jnp.sum(density.astype(jnp.float32) * potential, axis=0)
     total_points = point_rows * n

time: 178 us -> 120 us (0.67)
  waiting for transfers between devices: 24 us -> 0 us
  blocking collectives: 17.2 us -> 0 us
  Pallas kernels: 93.3 us -> 110 us
  starting transfers between devices: 13.7 us -> 0 us
  local copies, waits for them, and re-layouts: 17.9 us -> 9.08 us
  matrix products: 6.69 us -> 0 us
  other arithmetic: 4.16 us -> 0 us
    all_to_all x3 -> x0, waiting for transfers between devices: 24 us -> none  [the longest x2 15.1 us: gather_stacked(): lax.all_to_all(copies, 'pts', split_axis=0, concat_axis=0, tiled=True)]
    all_to_all x1 -> x0, blocking collectives: 17.2 us -> none  [gather_stacked(): lax.all_to_all(copies, 'pts', split_axis=0, concat_axis=0, tiled=True)]
    pallas_call x1, Pallas kernels: 93.3 us -> 110 us  [fused(): pl.pallas_call(functools.partial(fused_kernel, n, walker_count), out_shap...]
    all_to_all x3 -> x0, starting transfers between devices: 13.7 us -> none  [the longest x2 10.2 us: gather_stacked(): lax.all_to_all(copies, 'pts', split_axis=0, concat_axis=0, tiled=True)]
    dot_general x2 -> x0, matrix products: 6.69 us -> none  [the longest x1 4.17 us: body(): jnp.dot(core, jnp.moveaxis(gather_stacked(density.T), 2, 1).reshape(point...]
    transpose x4 -> x0, local copies, waits for them, and re-layouts: 4.18 us -> none  [the longest x1 2.3 us: body(): jnp.moveaxis(gather_stacked(field.T), 2, 1)]
    reduce_sum x3 -> x0, other arithmetic: 2.58 us -> none  [the longest x1 1.1 us: body(): exchange = jnp.sum(sums, axis=(1, 2))]
    convert_element_type x1 -> x0, local copies, waits for them, and re-layouts: 2.49 us -> none  [body(): orbit.astype(jnp.float32) * trial_here.astype(jnp.float32)[:, None, :]]
  transfers between devices with their start and end apart: 3 -> 0, of which waited for: 3 -> 0; matrix products, arithmetic and copies ran while one was open for 3% -> 0% of each run, Pallas kernels for 0% -> 0%
where the time goes in v1:
time: 120 us
  Pallas kernels  110 us (92%)
  local copies, waits for them, and re-layouts  9.08 us (8%)
    pallas_call x1, Pallas kernels, fused(): pl.pallas_call(functools.partial(fused_kernel, n, walker_count), out_shap...  110 us
    unnamed x2, local copies, waits for them, and re-layouts  3.93 us
    reshape x1, local copies, waits for them, and re-layouts, body(): flat_walkers = walkers.reshape(orbitals, walker_count * occupied)  2.78 us

profile of v1, /device:TPU:0, one launch (start us, length us, event | category | flops | bytes accessed | tf_op | source)
XLA Modules:
  0.0 120.0 jit_solution(14615740740744802279)
XLA Ops:
  0.6 3.2 %copy.9 = bf16[800,12,128]{0,2,1:T(8,128)(2,1)S(1)} copy(bf16[800,12,128]{2,0,1:T(8,128)(2,1)} %param.8) | data formatting | bytes 4915200 | tf_op args[3]
  3.9 2.8 %copy.10.walkers_hbm = bf16[800,1536]{1,0:T(8,128)(2,1)} copy(bf16[800,1536]{0,1:T(8,128)(2,1)S(1)} %bitcast.2) | data formatting | bytes 4915200 | tf_op jit(solution)/shard_map/reshape | solution.py:471
  6.6 110.3 %fused.1 = (bf16[50,1536]{1,0:T(8,128)(2,1)}, f32[16,128]{1,0:T(8,128)}) custom-call(bf16[400,800]{1,0:T(8,128)(2,1)} %map_hbm.1, bf16[6400,128]{1,0:T(8,128)(2,1)} %trial_hbm.1, bf16[400,6400]{1,0:T(8,128)(2,1)} %core_hbm.1, bf16[800,1536]{1,0:T(8,128)(2,1)} %copy.10.walkers_hbm, s32[12,400]{1,0:T(8,128)} %bitcast.3), custom_call_target="tpu_custom_call" | custom-call | tf_op jit(solution)/shard_map/fused/pallas_call | solution.py:342
  116.9 1.3 %slice_reduce_fusion = f32[12]{0:T(128)} fusion(f32[16,128]{1,0:T(8,128)} %get-tuple-element.5), kind=kLoop, calls=%fused_computation | loop fusion | bytes 96 | tf_op jit(solution)/shard_map/slice | solution.py:474
  118.2 1.0 reshape.11
  119.3 0.7 copy.11

commit v2 on v1

--- a/solution.py
+++ b/solution.py
@@ -31,7 +31,7 @@
 
 def fused_kernel(
     n, walker_count, map_hbm, trial_hbm, core_hbm, walkers_hbm, draws_ref, out_ref, energy_ref,
-    gathered, trial_ref, core_ref, walkers_ref, orbit_own, blocks, sums, total, term,
+    gathered, tails, trial_ref, core_ref, walkers_ref, orbit_own, blocks, sums, total, term,
     dens_own, dens_slots, dens_full, field_own, field_slots, fields, chosen, energy_own, energy_slots, pick, outgoing, incoming,
     local_sems, right_sems, left_sems, side_sems, recv_sems, dens_sems, field_sems, energy_sems, out_sems,
 ):
@@ -40,13 +40,16 @@
     own, orbitals = total.shape
     points = gathered.shape[0]
     window = blocks.shape[0]
-    own_rows = out_ref.shape[0]
+    own_rows = out_ref.shape[1]
     lines = dens_own.shape[0]
     span = chosen.shape[0]
     chips = n // 2
     far = chips // 2
     top = (rows // 2 + 15) // 16 * 16
     parts = ((0, top), (top, rows - top))
+    main = orbitals // LANES * LANES
+    rest = orbitals - main
+    fold = tails.shape[1]
     me = lax.axis_index("pts")
     core_id = lax.rem(me, 2)
     chip = me // 2
@@ -62,9 +65,11 @@
     def rows_of(index):
         return pl.ds(pl.multiple_of(index * rows, 16), rows)
 
-    def slot(index, part=None):
-        offset, length = (0, rows) if part is None else parts[part]
-        return gathered.at[pl.ds(pl.multiple_of(index * rows + offset, 16), length), :]
+    def slot(index, part):
+        if part == 2:
+            return tails.at[index]
+        offset, length = parts[part]
+        return gathered.at[pl.ds(pl.multiple_of(index * rows + offset, 16), length), 0:main]
 
     def remote(src, dst, send_sem, recv_sem, target):
         return pltpu.make_async_remote_copy(
@@ -77,13 +82,52 @@
         )
 
     def send(index, part, send_sem, target):
-        return remote(slot(index, part), slot(index, part), send_sem, recv_sems.at[index, part or 0], target)
-
-    def forward(index, part, send_sem, target):
-        send(index, part, send_sem, target).start()
-
-    def arrived(index, part=None):
-        send(index, part, side_sems.at[0, 0], partner).wait_recv()
+        return remote(slot(index, part), slot(index, part), send_sem, recv_sems.at[index, part], target)
+
+    def arrived(index, part):
+        send(index, part, side_sems.at[0, 0, 0], partner).wait_recv()
+
+    def unfold(index):
+        folded = tails[index].astype(jnp.float32)
+        for number, offset in enumerate(range(0, rows, fold)):
+            length = min(fold, rows - offset)
+            lined = pltpu.roll(folded, LANES - number * rest, 1) if number else folded
+            here = pl.ds(pl.multiple_of(index * rows + offset, 16), length)
+            gathered[here, main:orbitals] = lined[:length, :rest].astype(jnp.bfloat16)
+
+    def point(hop, chunk):
+        ahead, behind = device(ring + hop, core_id), device(ring - hop, core_id)
+        messages = ((0,), (1, 2))[chunk]
+
+        @pl.when(hop < far)
+        def _():
+            for message in messages:
+                arrived(behind, message)
+
+                @pl.when(jnp.logical_or(hop < far - 1, chunk == 0))
+                def _():
+                    send(behind, message, right_sems.at[hop, message], right).start()
+
+                send(behind, message, side_sems.at[0, hop, message], partner).start()
+            for message in messages:
+                arrived(ahead, message)
+
+                @pl.when(jnp.logical_or(hop < far - 1, chunk == 1))
+                def _():
+                    send(ahead, message, left_sems.at[hop, message], left).start()
+
+                send(ahead, message, side_sems.at[1, hop, message], partner).start()
+            if chunk == 1:
+                unfold(behind)
+                unfold(ahead)
+
+        @pl.when(hop == far)
+        def _():
+            for message in messages:
+                arrived(ahead, message)
+                send(ahead, message, side_sems.at[0, hop, message], partner).start()
+            if chunk == 1:
+                unfold(ahead)
 
     def to_everyone(source, slots, sems):
         for step in range(1, n):
@@ -103,27 +147,49 @@
     own_here = rows_of(me)
     local = [
         pltpu.make_async_copy(map_hbm, gathered.at[own_here, :], local_sems.at[0]),
-        pltpu.make_async_copy(walkers_hbm, walkers_ref, local_sems.at[1]),
-        pltpu.make_async_copy(trial_hbm, trial_ref, local_sems.at[2]),
-        pltpu.make_async_copy(core_hbm, core_ref, local_sems.at[3]),
+        pltpu.make_async_copy(trial_hbm, trial_ref, local_sems.at[1]),
+        pltpu.make_async_copy(core_hbm, core_ref, local_sems.at[2]),
     ]
-    for copy in local:
-        copy.start()
+    local[0].start()
+    slabs = [
+        pltpu.make_async_copy(
+            walkers_hbm.at[walker],
+            walkers_ref.at[:, walker * occupied : (walker + 1) * occupied],
+            local_sems.at[3 + walker],
+        )
+        for walker in range(walker_count)
+    ]
     barrier = pltpu.get_barrier_semaphore()
     for step in range(1, n):
         pl.semaphore_signal(
             barrier, inc=1, device_id={"pts": lax.rem(me + step, n)}, device_id_type=pl.DeviceIdType.MESH
         )
+    for copy in slabs + local[1:]:
+        copy.start()
     sums[...] = jnp.zeros_like(sums)
     total[...] = jnp.zeros_like(total)
     local[0].wait()
     pl.semaphore_wait(barrier, n - 1)
-    send(me, None, right_sems.at[0], right).start()
-    send(me, None, left_sems.at[0], left).start()
-    send(me, None, side_sems.at[0, 0], partner).start()
-
+    send(me, 0, right_sems.at[0, 0], right).start()
+    send(me, 0, left_sems.at[0, 0], left).start()
+    send(me, 0, side_sems.at[0, 0, 0], partner).start()
+    folded = jnp.zeros((fold, LANES), jnp.float32)
+    for number, offset in enumerate(range(0, rows, fold)):
+        length = min(fold, rows - offset)
+        place = (
+            lax.broadcasted_iota(jnp.int32, (rest, LANES), 0) + number * rest
+            == lax.broadcasted_iota(jnp.int32, (rest, LANES), 1)
+        ).astype(jnp.bfloat16)
+        here = pl.ds(pl.multiple_of(me * rows + offset, 16), length)
+        lined = dot(gathered[here, main:orbitals], place, (((1,), (0,)), ((), ())))
+        if length < fold:
+            lined = jnp.concatenate([lined, jnp.zeros((fold - length, LANES), jnp.float32)], axis=0)
+        folded = folded + lined
+    tails[me] = folded.astype(jnp.bfloat16)
+
+    for copy in slabs:
+        copy.wait()
     local[1].wait()
-    local[2].wait()
     orbit_own[...] = dot(gathered[own_here, :], walkers_ref[...], (((1,), (0,)), ((), ()))).astype(jnp.bfloat16)
     trial_own = trial_ref[own_here, :].astype(jnp.float32)
     lane = lax.broadcasted_iota(jnp.int32, (rows, LANES), 1)
@@ -148,6 +214,10 @@
     dens_own[...] = shifted
     dens_slots[me] = shifted
     to_everyone(lambda peer: dens_own, dens_slots, dens_sems)
+    for message in (1, 2):
+        send(me, message, right_sems.at[0, message], right).start()
+        send(me, message, left_sems.at[0, message], left).start()
+        send(me, message, side_sems.at[0, 0, message], partner).start()
 
     start = me * own
     left_col = pl.multiple_of(jnp.minimum(start // LANES * LANES, columns - 2 * LANES), LANES)
@@ -162,7 +232,7 @@
     out_row = lax.rem(out_line, outgoing.shape[1])
     wanted = jnp.where(out_row < own_rows, out_line // outgoing.shape[1] * own_rows + out_row, -1)
     pick[...] = (wanted == lax.broadcasted_iota(jnp.int32, pick.shape, 1)).astype(jnp.bfloat16)
-    local[3].wait()
+    local[2].wait()
 
     def exchange(pair, weight):
         first = pair * rows
@@ -181,59 +251,71 @@
             product = core_here * ahead_dot * back_dot
             sums[walker] += weight * jnp.sum(product.reshape(rows // 8, 8, window), axis=0)
 
+    owner = (start + lax.broadcasted_iota(jnp.int32, (own, 1), 0)) // occupied - start // occupied
+
+    def take_fields():
+        from_everyone(lambda peer: fields.at[pl.ds(peer * own // occupied, span)], field_slots, field_sems)
+        chosen[...] = jnp.zeros_like(chosen)
+        for index in range(n):
+            there = pl.ds(index * rows // LANES * LANES, window)
+            for line in range(span):
+                chosen[line, :, there] += field_slots[index, line]
+
+    def add_chip(where):
+        for side in range(2):
+            index = 2 * where + side
+            block = gathered[rows_of(index), :]
+            current = dot(term[...], block, CONTRACT_LAST).astype(jnp.bfloat16).astype(jnp.float32)
+            turn = lax.rem(window - lax.rem(index * rows, LANES), window)
+            lined = [pltpu.roll(field_slots[index, line], turn, 1)[:, :rows] for line in range(span)]
+            spread = lined[0]
+            for line in range(1, span):
+                spread = jnp.where(owner == line, lined[line], spread)
+            scaled = (spread * current).astype(jnp.bfloat16)
+            total[...] += dot(scaled, block, (((1,), (0,)), ((), ())))
+
     @pl.loop(0, 2 * far + 1)
     def _(task):
         hop = task // 2
         same = lax.rem(task, 2) == 0
-        ahead, behind = device(ring + hop, core_id), device(ring - hop, core_id)
-        ahead_side, behind_side = device(ring + hop, 1 - core_id), device(ring - hop, 1 - core_id)
         last = hop == far
-        middle = jnp.logical_and(hop > 0, hop < far)
-
-        @pl.when(jnp.logical_and(same, middle))
-        def _():
-            arrived(behind)
-
-            @pl.when(hop < far - 1)
+
+        @pl.when(jnp.logical_not(same))
+        def _():
+            point(hop + 1, 0)
+
+        @pl.when(jnp.logical_and(same, task > 0))
+        def _():
+            point(hop, 1)
+
+        ahead, ahead_side = device(ring + hop, core_id), device(ring + hop, 1 - core_id)
+        behind_side = device(ring - hop, 1 - core_id)
+
+        @pl.when(jnp.logical_or(jnp.logical_not(same), last))
+        def _():
+            for message in range(3):
+                arrived(ahead_side, message)
+            unfold(ahead_side)
+
+            @pl.when(jnp.logical_and(hop > 0, hop < far))
             def _():
-                forward(behind, None, right_sems.at[hop], right)
-
-            @pl.when(hop == far - 1)
-            def _():
-                forward(behind, 0, right_sems.at[hop], right)
-
-            forward(behind, None, side_sems.at[0, hop], partner)
-            arrived(ahead)
-
-            @pl.when(hop < far - 1)
-            def _():
-                forward(ahead, None, left_sems.at[hop], left)
-
-            @pl.when(hop == far - 1)
-            def _():
-                forward(ahead, 1, left_sems.at[hop], left)
-
-            forward(ahead, None, side_sems.at[1, hop], partner)
-
-        @pl.when(last)
-        def _():
-            for part in range(2):
-                arrived(ahead, part)
-                forward(ahead, part, side_sems.at[part, hop], partner)
-            for part in range(2):
-                arrived(ahead_side, part)
-
-        @pl.when(jnp.logical_not(same))
-        def _():
-            arrived(ahead_side)
-
-            @pl.when(hop > 0)
-            def _():
-                arrived(behind_side)
+                for message in range(3):
+                    arrived(behind_side, message)
+                unfold(behind_side)
 
         near = jnp.where(same, ahead, ahead_side)
         pair = jnp.where(jnp.logical_and(last, ring >= far), ahead_side, near)
         exchange(pair, jnp.where(hop == 0, 1.0, 2.0))
+
+        @pl.when(task == far)
+        def _():
+            take_fields()
+
+        @pl.when(task >= far)
+        def _():
+            late = task - far
+            away = (late + 1) // 2
+            add_chip(device(jnp.where(lax.rem(late, 2) == 1, ring + away, ring - away), 0) // 2)
 
         @pl.when(task == 1)
         def _():
@@ -259,18 +341,16 @@
     energy_own[:walker_count, :] = (energy_own[:walker_count, :] - walker_exchange / occupied) / (2.0 * points)
     energy_slots[me] = energy_own[...]
     to_everyone(lambda peer: energy_own, energy_slots, energy_sems)
-    from_everyone(lambda peer: fields.at[pl.ds(peer * own // occupied, span)], field_slots, field_sems)
-    chosen[...] = jnp.zeros_like(chosen)
-    for index in range(n):
-        there = pl.ds(index * rows // LANES * LANES, window)
-        for line in range(span):
-            chosen[line, :, there] += field_slots[index, line]
-
+    @pl.loop(far + 1, 2 * far)
+    def _(late):
+        away = (late + 1) // 2
+        add_chip(device(jnp.where(lax.rem(late, 2) == 1, ring + away, ring - away), 0) // 2)
+
+    term[...] = total[...].astype(jnp.bfloat16)
+    running = running + term[...].astype(jnp.float32)
     piece = next(p for p in (1280, 640, 256, points) if points % p == 0)
-    owner = (start + lax.broadcasted_iota(jnp.int32, (own, 1), 0)) // occupied - start // occupied
-    for degree in range(1, TAYLOR + 1):
-        if degree > 1:
-            total[...] = jnp.zeros_like(total)
+    for degree in range(2, TAYLOR + 1):
+        total[...] = jnp.zeros_like(total)
 
         @pl.loop(0, points // piece)
         def _(number):
@@ -309,7 +389,7 @@
                     moved = pltpu.roll(moved, offset % LANES, 1)
                 keep = jnp.logical_and(out_lane >= offset, out_lane < offset + own)
                 tile = jnp.where(keep, moved, tile)
-        out_ref[:, number * LANES : (number + 1) * LANES] = tile[:own_rows].astype(jnp.bfloat16)
+        out_ref[number] = tile[:own_rows].astype(jnp.bfloat16)
 
     all_sent(lambda peer: dens_own, dens_slots, dens_sems)
     all_sent(lambda peer: fields.at[pl.ds(peer * own // occupied, span)], field_slots, field_sems)
@@ -317,19 +397,20 @@
     all_sent(lambda peer: outgoing.at[peer], incoming, out_sems)
     for hop in range(far):
         for number, (sems, target) in enumerate(((right_sems, right), (left_sems, left))):
-            part = number if hop == far - 1 and hop > 0 else None
-            send(me, part, sems.at[hop], target).wait_send()
-    send(me, None, side_sems.at[0, 0], partner).wait_send()
-    for hop in range(1, far + 1):
-        for number in range(2):
-            part = number if hop == far else None
-            send(me, part, side_sems.at[number, hop], partner).wait_send()
-
-
-def fused(n, points_map, trial, core, flat_walkers, draws_t, walker_count):
+            for message in range(3) if hop < far - 1 else ((0,), (1, 2))[number]:
+                send(me, message, sems.at[hop, message], target).wait_send()
+    for hop in range(far + 1):
+        for number in range(2 if 0 < hop < far else 1):
+            for message in range(3):
+                send(me, message, side_sems.at[number, hop, message], partner).wait_send()
+
+
+def fused(n, points_map, trial, core, walker_major, draws_t):
     rows, orbitals = points_map.shape
     points, occupied = trial.shape
-    columns = flat_walkers.shape[1]
+    walker_count = walker_major.shape[0]
+    columns = walker_count * occupied
+    fold = (rows // (LANES // (orbitals % LANES)) + 15) // 16 * 16
     own, own_rows = columns // n, orbitals // n
     lines = (walker_count + 1 + 15) // 16 * 16
     span = (own + occupied - 2) // occupied + 1
@@ -342,13 +423,14 @@
     return pl.pallas_call(
         functools.partial(fused_kernel, n, walker_count),
         out_shape=(
-            jax.ShapeDtypeStruct((own_rows, columns), jnp.bfloat16),
+            jax.ShapeDtypeStruct((walker_count, own_rows, occupied), jnp.bfloat16),
             jax.ShapeDtypeStruct((lines, LANES), jnp.float32),
         ),
         in_specs=[pl.BlockSpec(memory_space=pl.ANY)] * 4 + [pl.BlockSpec(memory_space=pltpu.VMEM)],
         out_specs=[pl.BlockSpec(memory_space=pltpu.VMEM)] * 2,
         scratch_shapes=[
             vmem((points, orbitals), jnp.bfloat16),
+            vmem((n, fold, LANES), jnp.bfloat16),
             vmem((points, occupied), jnp.bfloat16),
             vmem((rows, points), jnp.bfloat16),
             vmem((orbitals, columns), jnp.bfloat16),
@@ -369,11 +451,11 @@
             vmem((n * height, orbitals), jnp.bfloat16),
             vmem((n, height, LANES), jnp.bfloat16),
             vmem((n, height, LANES), jnp.bfloat16),
-            dma((4,)),
-            dma((far,)),
-            dma((far,)),
-            dma((2, far + 1)),
-            dma((n, 2)),
+            dma((3 + walker_count,)),
+            dma((far, 3)),
+            dma((far, 3)),
+            dma((2, far + 1, 3)),
+            dma((n, 3)),
             dma((2, n)),
             dma((2, n)),
             dma((2, n)),
@@ -383,7 +465,7 @@
             collective_id=0, has_side_effects=True, vmem_limit_bytes=60 * 2**20
         ),
         name="fused",
-    )(points_map, trial, core, flat_walkers, draws_t)
+    )(points_map, trial, core, walker_major, draws_t)
 
 
 def propagate_kernel(n, occupied, piece, map_ref, field_ref, cols_ref, out_ref, wide, total, term):
@@ -468,10 +550,11 @@
     n = lax.axis_size("pts")
     own_rows = orbitals // n
     own_cols = walker_count * occupied // n
+    rest = orbitals % LANES
+    if point_rows % 16 == 0 and n % 8 == 0 and own_cols <= LANES and occupied == LANES and rest and LANES % rest == 0:
+        placed, energy = fused(n, points_map, trial, core, jnp.moveaxis(walkers, 1, 0), draws.T)
+        return jnp.moveaxis(placed, 0, 1), energy[:walker_count, 0]
     flat_walkers = walkers.reshape(orbitals, walker_count * occupied)
-    if point_rows % 16 == 0 and n % 8 == 0 and own_cols <= LANES and occupied == LANES:
-        placed, energy = fused(n, points_map, trial, core, flat_walkers, draws.T, walker_count)
-        return placed.reshape(own_rows, walker_count, occupied), energy[:walker_count, 0]
     point_first = lax.axis_index("pts") * point_rows
     trial_here = lax.dynamic_slice_in_dim(trial, point_first, point_rows, 0)
     flat_orbit = jnp.dot(points_map, flat_walkers, preferred_element_type=jnp.float32).astype(jnp.bfloat16)

time: 120 us -> 105 us (0.88)
  Pallas kernels: 110 us -> 101 us
  local copies, waits for them, and re-layouts: 9.08 us -> 2.92 us
    pallas_call x1, Pallas kernels: 110 us -> 101 us  [fused(): pl.pallas_call(functools.partial(fused_kernel, n, walker_count), out_shap...]
    reshape x2 -> x0, local copies, waits for them, and re-layouts: 3.83 us -> none  [the longest x1 2.78 us: body(): flat_walkers = walkers.reshape(orbitals, walker_count * occupied)]
    unnamed x2 -> x1, local copies, waits for them, and re-layouts: 3.93 us -> 1.6 us
where the time goes in v2:
time: 105 us; the launch traced here: 104 us
  Pallas kernels  101 us (96%)
  local copies, waits for them, and re-layouts  2.92 us (3%)
    pallas_call x1, Pallas kernels, fused(): pl.pallas_call(functools.partial(fused_kernel, n, walker_count), out_shap...  101 us

profile of v2, /device:TPU:0, one launch (start us, length us, event | category | flops | bytes accessed | tf_op | source)
XLA Modules:
  0.0 104.2 jit_solution(14218992226713986820)
XLA Ops:
  0.6 100.6 %fused.1 = (bf16[12,50,128]{2,1,0:T(8,128)(2,1)}, f32[16,128]{1,0:T(8,128)}) custom-call(bf16[400,800]{1,0:T(8,128)(2,1)} %map_hbm.1, bf16[6400,128]{1,0:T(8,128)(2,1)} %trial_hbm.1, bf16[400,6400]{1,0:T(8,128)(2,1)} %core_hbm.1, bf16[12,800,128]{2,1,0:T(8,128)(2,1)} %bitcast.3, s32[12,400]{1,0:T(8,128)} %bitcast.5), custom_call_target="tpu_custom_call" | custom-call | tf_op jit(solution)/shard_map/fused/pallas_call | solution.py:423
  101.2 1.3 %slice_reduce_fusion = f32[12]{0:T(128)} fusion(f32[16,128]{1,0:T(8,128)} %get-tuple-element.5), kind=kLoop, calls=%fused_computation | loop fusion | bytes 96 | tf_op jit(solution)/shard_map/slice | solution.py:556
  102.6 1.6 %copy.8 = bf16[50,12,128]{2,0,1:T(8,128)(2,1)} copy(bf16[50,12,128]{2,0,1:T(8,128)(2,1)} %bitcast.4) | data formatting | bytes 307200

commit v3 on v2

--- a/solution.py
+++ b/solution.py
@@ -33,7 +33,7 @@
     n, walker_count, map_hbm, trial_hbm, core_hbm, walkers_hbm, draws_ref, out_ref, energy_ref,
     gathered, tails, trial_ref, core_ref, walkers_ref, orbit_own, blocks, sums, total, term,
     dens_own, dens_slots, dens_full, field_own, field_slots, fields, chosen, energy_own, energy_slots, pick, outgoing, incoming,
-    local_sems, right_sems, left_sems, side_sems, recv_sems, dens_sems, field_sems, energy_sems, out_sems,
+    local_sems, in_sems, out_sems_map, across_sems, side_sems, recv_sems, dens_sems, field_sems, energy_sems, out_sems,
 ):
     rows, columns = orbit_own.shape
     occupied = trial_ref.shape[1]
@@ -41,6 +41,8 @@
     points = gathered.shape[0]
     window = blocks.shape[0]
     own_rows = out_ref.shape[1]
+    half = LANES // 2
+    height = pick.shape[0] // n
     lines = dens_own.shape[0]
     span = chosen.shape[0]
     chips = n // 2
@@ -60,7 +62,20 @@
         where = jnp.where(place < far, 2 * place, 2 * (chips - 1 - place) + 1)
         return 2 * where + side
 
-    right, left, partner = device(ring + 1, core_id), device(ring - 1, core_id), device(ring, 1 - core_id)
+    quarter = lax.rem(ring, 4)
+    is_middle = jnp.logical_or(quarter == 1, quarter == 2)
+    is_corner = jnp.logical_not(is_middle)
+    sign = jnp.where(quarter < 2, 1, -1)
+    steps = (0, sign, -sign, 2 * sign, -2 * sign, 3 * sign, far, -3 * sign)
+    inner, outer = device(ring + sign, core_id), device(ring - sign, core_id)
+    across, partner = device(chips - 1 - ring, core_id), device(ring, 1 - core_id)
+
+    def near(which, side):
+        return device(ring + steps[which], side)
+
+    def share(which):
+        other = lax.rem(ring + steps[which] + 2 * chips, chips)
+        return device(other, jnp.where(ring < other, core_id, 1 - core_id))
 
     def rows_of(index):
         return pl.ds(pl.multiple_of(index * rows, 16), rows)
@@ -85,7 +100,7 @@
         return remote(slot(index, part), slot(index, part), send_sem, recv_sems.at[index, part], target)
 
     def arrived(index, part):
-        send(index, part, side_sems.at[0, 0, 0], partner).wait_recv()
+        send(index, part, side_sems.at[0, 0], partner).wait_recv()
 
     def unfold(index):
         folded = tails[index].astype(jnp.float32)
@@ -95,39 +110,84 @@
             here = pl.ds(pl.multiple_of(index * rows + offset, 16), length)
             gathered[here, main:orbitals] = lined[:length, :rest].astype(jnp.bfloat16)
 
-    def point(hop, chunk):
-        ahead, behind = device(ring + hop, core_id), device(ring - hop, core_id)
+    def go(which, message, sems, number, target):
+        send(near(which, core_id), message, sems.at[number, message], target).start()
+
+    def land(which, message):
+        arrived(near(which, core_id), message)
+        go(which, message, side_sems, which, partner)
+
+    def point(stage, chunk):
         messages = ((0,), (1, 2))[chunk]
-
-        @pl.when(hop < far)
-        def _():
+        if stage == 1:
             for message in messages:
-                arrived(behind, message)
-
-                @pl.when(jnp.logical_or(hop < far - 1, chunk == 0))
+                land(1, message)
+                go(1, message, out_sems_map, 1, outer)
+                land(2, message)
+                go(2, message, in_sems, 1, inner)
+
+                @pl.when(is_middle)
                 def _():
-                    send(behind, message, right_sems.at[hop, message], right).start()
-
-                send(behind, message, side_sems.at[0, hop, message], partner).start()
+                    go(1, message, across_sems, 1, across)
+                    land(7, message)
+
+            if chunk == 1:
+                unfold(near(1, core_id))
+                unfold(near(2, core_id))
+
+                @pl.when(is_middle)
+                def _():
+                    unfold(near(7, core_id))
+
+        if stage == 2:
             for message in messages:
-                arrived(ahead, message)
-
-                @pl.when(jnp.logical_or(hop < far - 1, chunk == 1))
+                land(3, message)
+                go(3, message, out_sems_map, 2, outer)
+                land(4, message)
+
+                @pl.when(is_middle)
                 def _():
-                    send(ahead, message, left_sems.at[hop, message], left).start()
-
-                send(ahead, message, side_sems.at[1, hop, message], partner).start()
+                    if chunk == 0:
+                        go(4, message, in_sems, 2, inner)
+                    else:
+                        go(3, message, across_sems, 2, across)
+                    land(6, message)
+
             if chunk == 1:
-                unfold(behind)
-                unfold(ahead)
-
-        @pl.when(hop == far)
-        def _():
+                unfold(near(3, core_id))
+                unfold(near(4, core_id))
+
+                @pl.when(is_middle)
+                def _():
+                    unfold(near(6, core_id))
+
+        if stage == 3:
             for message in messages:
-                arrived(ahead, message)
-                send(ahead, message, side_sems.at[0, hop, message], partner).start()
+                land(5, message)
+
+                @pl.when(is_corner)
+                def _():
+                    go(5, message, out_sems_map, 3, outer)
+                    land(7, message)
+
             if chunk == 1:
-                unfold(ahead)
+                unfold(near(5, core_id))
+
+                @pl.when(is_corner)
+                def _():
+                    unfold(near(7, core_id))
+
+        if stage == 4:
+            for message in messages:
+                land(6, message)
+            if chunk == 1:
+                unfold(near(6, core_id))
+
+    def land_side(which):
+        index = near(which, 1 - core_id)
+        for message in range(3):
+            arrived(index, message)
+        unfold(index)
 
     def to_everyone(source, slots, sems):
         for step in range(1, n):
@@ -143,6 +203,24 @@
         for step in range(1, n):
             peer = lax.rem(me + step, n)
             remote(source(peer), slots.at[me], sems.at[0, step], sems.at[1, me], peer).wait_send()
+
+    middle_first = n // 4
+
+    def low_of(number):
+        return number * own // occupied
+
+    def each_middle(act):
+        for number in range(n // 2):
+
+            @pl.when(me != middle_first + number)
+            def _():
+                act(number, middle_first + number)
+
+    def field_send(number, peer):
+        return remote(
+            fields.at[pl.ds(low_of(number), span)], field_slots.at[me], field_sems.at[0, number],
+            field_sems.at[1, me], peer,
+        )
 
     own_here = rows_of(me)
     local = [
@@ -170,9 +248,17 @@
     total[...] = jnp.zeros_like(total)
     local[0].wait()
     pl.semaphore_wait(barrier, n - 1)
-    send(me, 0, right_sems.at[0, 0], right).start()
-    send(me, 0, left_sems.at[0, 0], left).start()
-    send(me, 0, side_sems.at[0, 0, 0], partner).start()
+    def start_own(message):
+        go(0, message, in_sems, 0, inner)
+        go(0, message, out_sems_map, 0, outer)
+
+        @pl.when(is_middle)
+        def _():
+            go(0, message, across_sems, 0, across)
+
+        go(0, message, side_sems, 0, partner)
+
+    start_own(0)
     folded = jnp.zeros((fold, LANES), jnp.float32)
     for number, offset in enumerate(range(0, rows, fold)):
         length = min(fold, rows - offset)
@@ -215,11 +301,10 @@
     dens_slots[me] = shifted
     to_everyone(lambda peer: dens_own, dens_slots, dens_sems)
     for message in (1, 2):
-        send(me, message, right_sems.at[0, message], right).start()
-        send(me, message, left_sems.at[0, message], left).start()
-        send(me, message, side_sems.at[0, 0, message], partner).start()
-
-    start = me * own
+        start_own(message)
+
+    mine = jnp.clip(me - middle_first, 0, n // 2 - 1)
+    start = mine * own
     left_col = pl.multiple_of(jnp.minimum(start // LANES * LANES, columns - 2 * LANES), LANES)
     choose = (
         lax.broadcasted_iota(jnp.int32, (own, 2 * LANES), 0) + (start - left_col)
@@ -227,10 +312,9 @@
     ).astype(jnp.bfloat16)
     cols_own = dot(choose, walkers_ref[:, pl.ds(left_col, 2 * LANES)], CONTRACT_LAST).astype(jnp.bfloat16)
     term[...] = cols_own
-    running = cols_own.astype(jnp.float32)
     out_line = lax.broadcasted_iota(jnp.int32, pick.shape, 0)
-    out_row = lax.rem(out_line, outgoing.shape[1])
-    wanted = jnp.where(out_row < own_rows, out_line // outgoing.shape[1] * own_rows + out_row, -1)
+    out_row = lax.rem(out_line, height)
+    wanted = jnp.where(out_row < own_rows, out_line // height * own_rows + out_row, -1)
     pick[...] = (wanted == lax.broadcasted_iota(jnp.int32, pick.shape, 1)).astype(jnp.bfloat16)
     local[2].wait()
 
@@ -239,9 +323,17 @@
         block_base, block_shift = placed(pair)
         block_shift = pl.multiple_of(block_shift, 16)
         blocks[...] = jnp.zeros_like(blocks)
-        blocks[pl.ds(block_shift, rows), :] = dot(
-            gathered[rows_of(pair), :], walkers_ref[...], (((1,), (0,)), ((), ()))
-        ).astype(jnp.bfloat16)
+
+        @pl.when(pair == me)
+        def _():
+            blocks[pl.ds(block_shift, rows), :] = orbit_own[...]
+
+        @pl.when(pair != me)
+        def _():
+            blocks[pl.ds(block_shift, rows), :] = dot(
+                gathered[rows_of(pair), :], walkers_ref[...], (((1,), (0,)), ((), ()))
+            ).astype(jnp.bfloat16)
+
         core_here = core_ref[:, pl.ds(block_base, window)].astype(jnp.float32)
         trial_there = trial_ref[pl.ds(block_base, window), :]
         for walker in range(walker_count):
@@ -254,14 +346,19 @@
     owner = (start + lax.broadcasted_iota(jnp.int32, (own, 1), 0)) // occupied - start // occupied
 
     def take_fields():
-        from_everyone(lambda peer: fields.at[pl.ds(peer * own // occupied, span)], field_slots, field_sems)
+        for step in range(1, n):
+            peer = lax.rem(me + step, n)
+            remote(
+                fields.at[pl.ds(0, span)], field_slots.at[peer], field_sems.at[0, 0], field_sems.at[1, peer], peer
+            ).wait_recv()
         chosen[...] = jnp.zeros_like(chosen)
         for index in range(n):
             there = pl.ds(index * rows // LANES * LANES, window)
             for line in range(span):
                 chosen[line, :, there] += field_slots[index, line]
 
-    def add_chip(where):
+    def add_chip(which):
+        where = near(which, 0) // 2
         for side in range(2):
             index = 2 * where + side
             block = gathered[rows_of(index), :]
@@ -274,50 +371,64 @@
             scaled = (spread * current).astype(jnp.bfloat16)
             total[...] += dot(scaled, block, (((1,), (0,)), ((), ())))
 
-    @pl.loop(0, 2 * far + 1)
+    corner_list = (
+        me, partner, near(1, core_id), near(1, 1 - core_id), share(2), near(3, core_id), near(3, 1 - core_id),
+        near(4, core_id), near(4, 1 - core_id), near(7, core_id), near(7, 1 - core_id), share(5), share(6),
+    )
+    middle_list = {0: me, 1: partner, 3: share(1), 4: share(7), 7: share(6)}
+    stops = {1: (1, 0), 2: (1, 1), 4: (2, 0), 5: (2, 1), 8: (3, 0), 9: (3, 1)}
+    corner_stops = {11: (4, 0), 12: (4, 1)}
+    sides = {1: ((0,), ()), 3: ((1, 2), (7,)), 6: ((3, 4), (6,)), 10: ((5,), ())}
+    corner_sides = {10: (7,), 12: (6,)}
+    adds = {5: (0, 1), 6: (2, 7), 8: (3, 4, 6)}
+
+    @pl.loop(0, len(corner_list))
     def _(task):
-        hop = task // 2
-        same = lax.rem(task, 2) == 0
-        last = hop == far
-
-        @pl.when(jnp.logical_not(same))
+        for number, (stage, chunk) in stops.items():
+
+            @pl.when(task == number)
+            def _():
+                point(stage, chunk)
+
+        for number, (stage, chunk) in corner_stops.items():
+
+            @pl.when(jnp.logical_and(task == number, is_corner))
+            def _():
+                point(stage, chunk)
+
+        for number, (both, middle) in sides.items():
+
+            @pl.when(task == number)
+            def _():
+                for which in both:
+                    land_side(which)
+
+                @pl.when(is_middle)
+                def _():
+                    for which in middle:
+                        land_side(which)
+
+        for number, those in corner_sides.items():
+
+            @pl.when(jnp.logical_and(task == number, is_corner))
+            def _():
+                for which in those:
+                    land_side(which)
+
+        pair = me
+        active = is_corner
+        for number, choice in enumerate(corner_list):
+            pair = jnp.where(task == number, choice, pair)
+        for number, choice in middle_list.items():
+            hit = jnp.logical_and(task == number, is_middle)
+            pair = jnp.where(hit, choice, pair)
+            active = jnp.logical_or(active, hit)
+
+        @pl.when(active)
         def _():
-            point(hop + 1, 0)
-
-        @pl.when(jnp.logical_and(same, task > 0))
-        def _():
-            point(hop, 1)
-
-        ahead, ahead_side = device(ring + hop, core_id), device(ring + hop, 1 - core_id)
-        behind_side = device(ring - hop, 1 - core_id)
-
-        @pl.when(jnp.logical_or(jnp.logical_not(same), last))
-        def _():
-            for message in range(3):
-                arrived(ahead_side, message)
-            unfold(ahead_side)
-
-            @pl.when(jnp.logical_and(hop > 0, hop < far))
-            def _():
-                for message in range(3):
-                    arrived(behind_side, message)
-                unfold(behind_side)
-
-        near = jnp.where(same, ahead, ahead_side)
-        pair = jnp.where(jnp.logical_and(last, ring >= far), ahead_side, near)
-        exchange(pair, jnp.where(hop == 0, 1.0, 2.0))
-
-        @pl.when(task == far)
-        def _():
-            take_fields()
-
-        @pl.when(task >= far)
-        def _():
-            late = task - far
-            away = (late + 1) // 2
-            add_chip(device(jnp.where(lax.rem(late, 2) == 1, ring + away, ring - away), 0) // 2)
-
-        @pl.when(task == 1)
+            exchange(pair, jnp.where(task < 2, 1.0, 2.0))
+
+        @pl.when(task == 2)
         def _():
             from_everyone(lambda peer: dens_own, dens_slots, dens_sems)
             dens_full[...] = jnp.zeros_like(dens_full)
@@ -334,75 +445,118 @@
             turned = pltpu.roll(field_own[...], shift, 1)
             for line in range(walker_count):
                 fields[line] = turned[line : line + 1]
-            to_everyone(lambda peer: fields.at[pl.ds(peer * own // occupied, span)], field_slots, field_sems)
+            each_middle(lambda number, peer: field_send(number, peer).start())
             field_slots[me] = fields[pl.ds(start // occupied, span)]
+
+        @pl.when(jnp.logical_and(task == 5, is_middle))
+        def _():
+            take_fields()
+
+        for number, those in adds.items():
+
+            @pl.when(jnp.logical_and(task == number, is_middle))
+            def _():
+                for which in those:
+                    add_chip(which)
+
 
     walker_exchange = jnp.sum(jnp.sum(sums[...], axis=1), axis=1, keepdims=True)
     energy_own[:walker_count, :] = (energy_own[:walker_count, :] - walker_exchange / occupied) / (2.0 * points)
     energy_slots[me] = energy_own[...]
     to_everyone(lambda peer: energy_own, energy_slots, energy_sems)
-    @pl.loop(far + 1, 2 * far)
-    def _(late):
-        away = (late + 1) // 2
-        add_chip(device(jnp.where(lax.rem(late, 2) == 1, ring + away, ring - away), 0) // 2)
-
-    term[...] = total[...].astype(jnp.bfloat16)
-    running = running + term[...].astype(jnp.float32)
     piece = next(p for p in (1280, 640, 256, points) if points % p == 0)
-    for degree in range(2, TAYLOR + 1):
-        total[...] = jnp.zeros_like(total)
-
-        @pl.loop(0, points // piece)
-        def _(number):
-            here = pl.ds(pl.multiple_of(number * piece, piece), piece)
-            block = gathered[here, :]
-            current = dot(term[...], block, CONTRACT_LAST).astype(jnp.bfloat16).astype(jnp.float32)
-            spread = chosen[0, :, here]
-            for line in range(1, span):
-                spread = jnp.where(owner == line, chosen[line, :, here], spread)
-            scaled = (spread * current).astype(jnp.bfloat16)
-            total[...] += dot(scaled, block, (((1,), (0,)), ((), ())))
-
-        term[...] = (total[...] / degree).astype(jnp.bfloat16)
+
+    @pl.when(is_middle)
+    def _():
+        add_chip(5)
+        running = term[...].astype(jnp.float32)
+        term[...] = total[...].astype(jnp.bfloat16)
         running = running + term[...].astype(jnp.float32)
-
-    picked = dot(pick[...], running.astype(jnp.bfloat16), CONTRACT_LAST)
-    height = outgoing.shape[1]
-    for index in range(n):
-        outgoing[index, :, :own] = picked[index * height : (index + 1) * height].astype(jnp.bfloat16)
-    to_everyone(lambda peer: outgoing.at[peer], incoming, out_sems)
-    incoming[me] = outgoing[me]
+        for degree in range(2, TAYLOR + 1):
+            total[...] = jnp.zeros_like(total)
+
+            @pl.loop(0, points // piece)
+            def _(number):
+                here = pl.ds(pl.multiple_of(number * piece, piece), piece)
+                block = gathered[here, :]
+                current = dot(term[...], block, CONTRACT_LAST).astype(jnp.bfloat16).astype(jnp.float32)
+                spread = chosen[0, :, here]
+                for line in range(1, span):
+                    spread = jnp.where(owner == line, chosen[line, :, here], spread)
+                scaled = (spread * current).astype(jnp.bfloat16)
+                total[...] += dot(scaled, block, (((1,), (0,)), ((), ())))
+
+            term[...] = (total[...] / degree).astype(jnp.bfloat16)
+            running = running + term[...].astype(jnp.float32)
+        final = running.astype(jnp.bfloat16)
+        first = dot(pick[...], final[:LANES], CONTRACT_LAST)
+        padded = jnp.concatenate([final[LANES:], jnp.zeros((half, orbitals), jnp.bfloat16)], axis=0)
+        second = dot(pick[...], padded, CONTRACT_LAST)
+        for index in range(n):
+            upper = second[index * height : index * height + height // 2]
+            lower = second[index * height + height // 2 : (index + 1) * height]
+            outgoing[index, :height] = first[index * height : (index + 1) * height].astype(jnp.bfloat16)
+            outgoing[index, height:] = (upper + pltpu.roll(lower, half, 1)).astype(jnp.bfloat16)
+        for step in range(1, n):
+            peer = lax.rem(me + step, n)
+            remote(outgoing.at[peer], incoming.at[mine], out_sems.at[0, step], out_sems.at[1, mine], peer).start()
+        incoming[mine] = outgoing[me]
+
     from_everyone(lambda peer: energy_own, energy_slots, energy_sems)
     energy = energy_slots[0]
     for index in range(1, n):
         energy = energy + energy_slots[index]
     energy_ref[...] = energy
-    from_everyone(lambda peer: outgoing.at[peer], incoming, out_sems)
+    each_middle(
+        lambda number, peer: remote(
+            outgoing.at[0], incoming.at[number], out_sems.at[0, 0], out_sems.at[1, number], peer
+        ).wait_recv()
+    )
     out_lane = lax.broadcasted_iota(jnp.int32, (height, LANES), 1)
-    for number in range(columns // LANES):
-        tile = jnp.zeros((height, LANES), jnp.float32)
-        for index in range(n):
-            offset = index * own - number * LANES
-            if -own < offset < LANES:
-                moved = incoming[index].astype(jnp.float32)
-                if offset % LANES:
-                    moved = pltpu.roll(moved, offset % LANES, 1)
-                keep = jnp.logical_and(out_lane >= offset, out_lane < offset + own)
-                tile = jnp.where(keep, moved, tile)
-        out_ref[number] = tile[:own_rows].astype(jnp.bfloat16)
+    pieces = []
+    for number in range(n // 2):
+        got = incoming[number].astype(jnp.float32)
+        top_part, low_part = got[:height], got[height:]
+        pieces.append((top_part, 0))
+        pieces.append((top_part, 1))
+        pieces.append((jnp.concatenate([low_part, pltpu.roll(low_part, half, 1)], axis=0), 0))
+    for number in range(walker_count):
+        (low, low_at), (high, high_at) = pieces[2 * number], pieces[2 * number + 1]
+        low = pltpu.roll(low, half, 1) if low_at == 1 else low
+        high = pltpu.roll(high, half, 1) if high_at == 0 else high
+        out_ref[number] = jnp.where(out_lane < half, low, high)[:own_rows].astype(jnp.bfloat16)
 
     all_sent(lambda peer: dens_own, dens_slots, dens_sems)
-    all_sent(lambda peer: fields.at[pl.ds(peer * own // occupied, span)], field_slots, field_sems)
     all_sent(lambda peer: energy_own, energy_slots, energy_sems)
-    all_sent(lambda peer: outgoing.at[peer], incoming, out_sems)
-    for hop in range(far):
-        for number, (sems, target) in enumerate(((right_sems, right), (left_sems, left))):
-            for message in range(3) if hop < far - 1 else ((0,), (1, 2))[number]:
-                send(me, message, sems.at[hop, message], target).wait_send()
-    for hop in range(far + 1):
-        for number in range(2 if 0 < hop < far else 1):
-            for message in range(3):
-                send(me, message, side_sems.at[number, hop, message], partner).wait_send()
+    each_middle(lambda number, peer: field_send(number, peer).wait_send())
+
+    def sent(sems, number, messages, target):
+        for message in messages:
+            send(me, message, sems.at[number, message], target).wait_send()
+
+    for number in range(2):
+        sent(in_sems, number, range(3), inner)
+    for number in range(3):
+        sent(out_sems_map, number, range(3), outer)
+    for number in range(7):
+        sent(side_sems, number, range(3), partner)
+    sent(side_sems, 7, range(3), partner)
+
+    @pl.when(is_middle)
+    def _():
+        sent(in_sems, 2, (0,), inner)
+        sent(across_sems, 0, range(3), across)
+        sent(across_sems, 1, range(3), across)
+        sent(across_sems, 2, (1, 2), across)
+        for step in range(1, n):
+            peer = lax.rem(me + step, n)
+            remote(
+                outgoing.at[peer], incoming.at[mine], out_sems.at[0, step], out_sems.at[1, mine], peer
+            ).wait_send()
+
+    @pl.when(is_corner)
+    def _():
+        sent(out_sems_map, 3, range(3), outer)
 
 
 def fused(n, points_map, trial, core, walker_major, draws_t):
@@ -411,10 +565,10 @@
     walker_count = walker_major.shape[0]
     columns = walker_count * occupied
     fold = (rows // (LANES // (orbitals % LANES)) + 15) // 16 * 16
-    own, own_rows = columns // n, orbitals // n
+    own, own_rows = columns // (n // 2), orbitals // n
     lines = (walker_count + 1 + 15) // 16 * 16
-    span = (own + occupied - 2) // occupied + 1
-    height = (own_rows + 15) // 16 * 16
+    span = max((k * own + own - 1) // occupied - k * own // occupied + 1 for k in range(n // 2))
+    height = (own_rows + 31) // 32 * 32
     window = (rows + (LANES - 16) + LANES - 1) // LANES * LANES
     full = (points - rows) // LANES * LANES + window
     far = n // 4
@@ -449,12 +603,13 @@
             vmem((lines, LANES), jnp.float32),
             vmem((n, lines, LANES), jnp.float32),
             vmem((n * height, orbitals), jnp.bfloat16),
-            vmem((n, height, LANES), jnp.bfloat16),
-            vmem((n, height, LANES), jnp.bfloat16),
+            vmem((n, height + height // 2, LANES), jnp.bfloat16),
+            vmem((n // 2, height + height // 2, LANES), jnp.bfloat16),
             dma((3 + walker_count,)),
-            dma((far, 3)),
-            dma((far, 3)),
-            dma((2, far + 1, 3)),
+            dma((3, 3)),
+            dma((4, 3)),
+            dma((3, 3)),
+            dma((8, 3)),
             dma((n, 3)),
             dma((2, n)),
             dma((2, n)),
@@ -551,7 +706,7 @@
     own_rows = orbitals // n
     own_cols = walker_count * occupied // n
     rest = orbitals % LANES
-    if point_rows % 16 == 0 and n % 8 == 0 and own_cols <= LANES and occupied == LANES and rest and LANES % rest == 0:
+    if point_rows % 16 == 0 and n == 16 and 4 * own_cols == 3 * LANES and occupied == LANES and rest and LANES % rest == 0:
         placed, energy = fused(n, points_map, trial, core, jnp.moveaxis(walkers, 1, 0), draws.T)
         return jnp.moveaxis(placed, 0, 1), energy[:walker_count, 0]
     flat_walkers = walkers.reshape(orbitals, walker_count * occupied)

time: 105 us -> 90.5 us (0.86)
  Pallas kernels: 101 us -> 86.7 us
    pallas_call x1, Pallas kernels: 101 us -> 86.7 us  [fused(): pl.pallas_call(functools.partial(fused_kernel, n, walker_count), out_shap...]
where the time goes in v3:
time: 90.5 us; the launch traced here: 90.3 us
  Pallas kernels  86.7 us (96%)
  local copies, waits for them, and re-layouts  2.92 us (3%)
    pallas_call x1, Pallas kernels, fused(): pl.pallas_call(functools.partial(fused_kernel, n, walker_count), out_shap...  86.7 us

profile of v3, /device:TPU:0, one launch (start us, length us, event | category | flops | bytes accessed | tf_op | source)
XLA Modules:
  0.0 90.3 jit_solution(4988649355890640044)
XLA Ops:
  0.6 86.7 %fused.1 = (bf16[12,50,128]{2,1,0:T(8,128)(2,1)}, f32[16,128]{1,0:T(8,128)}) custom-call(bf16[400,800]{1,0:T(8,128)(2,1)} %map_hbm.1, bf16[6400,128]{1,0:T(8,128)(2,1)} %trial_hbm.1, bf16[400,6400]{1,0:T(8,128)(2,1)} %core_hbm.1, bf16[12,800,128]{2,1,0:T(8,128)(2,1)} %bitcast.3, s32[12,400]{1,0:T(8,128)} %bitcast.5), custom_call_target="tpu_custom_call" | custom-call | tf_op jit(solution)/shard_map/fused/pallas_call | solution.py:577
  87.3 1.3 %slice_reduce_fusion = f32[12]{0:T(128)} fusion(f32[16,128]{1,0:T(8,128)} %get-tuple-element.5), kind=kLoop, calls=%fused_computation | loop fusion | bytes 96 | tf_op jit(solution)/shard_map/slice | solution.py:711
  88.7 1.6 %copy.8 = bf16[50,12,128]{2,0,1:T(8,128)(2,1)} copy(bf16[50,12,128]{2,0,1:T(8,128)(2,1)} %bitcast.4) | data formatting | bytes 307200

commit v4 on v3

--- a/solution.py
+++ b/solution.py
@@ -30,21 +30,23 @@
 
 
 def fused_kernel(
-    n, walker_count, map_hbm, trial_hbm, core_hbm, walkers_hbm, draws_ref, out_ref, energy_ref,
-    gathered, tails, trial_ref, core_ref, walkers_ref, orbit_own, blocks, sums, total, term,
-    dens_own, dens_slots, dens_full, field_own, field_slots, fields, chosen, energy_own, energy_slots, pick, outgoing, incoming,
-    local_sems, in_sems, out_sems_map, across_sems, side_sems, recv_sems, dens_sems, field_sems, energy_sems, out_sems,
+    n, walker_count, own, map_hbm, trial_hbm, core_hbm, walkers_hbm, draws_ref, out_ref, energy_ref,
+    gathered, tails, trial_ref, core_ref, walkers_ref, orbit_own, blocks, sums, turned_map, gram, shared_gram, whole_half, shared_half,
+    dens_own, dens_slots, dens_full, field_own, field_slots, fields, energy_own, energy_slots, pick, outgoing, incoming,
+    local_sems, in_sems, out_sems_map, across_sems, side_sems, recv_sems, dens_sems, field_sems, energy_sems, out_sems, gram_sems,
 ):
     rows, columns = orbit_own.shape
     occupied = trial_ref.shape[1]
-    own, orbitals = total.shape
+    orbitals = gram.shape[0]
     points = gathered.shape[0]
     window = blocks.shape[0]
     own_rows = out_ref.shape[1]
     half = LANES // 2
     height = pick.shape[0] // n
     lines = dens_own.shape[0]
-    span = chosen.shape[0]
+    span = field_slots.shape[1]
+    width = 2 * LANES
+    split = (orbitals // LANES * LANES) - width
     chips = n // 2
     far = chips // 2
     top = (rows // 2 + 15) // 16 * 16
@@ -161,27 +163,13 @@
                 def _():
                     unfold(near(6, core_id))
 
-        if stage == 3:
-            for message in messages:
-                land(5, message)
-
-                @pl.when(is_corner)
-                def _():
-                    go(5, message, out_sems_map, 3, outer)
-                    land(7, message)
-
-            if chunk == 1:
-                unfold(near(5, core_id))
-
-                @pl.when(is_corner)
-                def _():
-                    unfold(near(7, core_id))
-
-        if stage == 4:
-            for message in messages:
-                land(6, message)
-            if chunk == 1:
-                unfold(near(6, core_id))
+    def far_point(which, chunk, onward):
+        for message in ((0,), (1, 2))[chunk]:
+            land(which, message)
+            if onward:
+                go(which, message, out_sems_map, 3, outer)
+        if chunk == 1:
+            unfold(near(which, core_id))
 
     def land_side(which):
         index = near(which, 1 - core_id)
@@ -245,7 +233,8 @@
     for copy in slabs + local[1:]:
         copy.start()
     sums[...] = jnp.zeros_like(sums)
-    total[...] = jnp.zeros_like(total)
+    gram[...] = jnp.zeros_like(gram)
+    shared_gram[...] = jnp.zeros_like(shared_gram)
     local[0].wait()
     pl.semaphore_wait(barrier, n - 1)
     def start_own(message):
@@ -299,19 +288,34 @@
     shifted = pltpu.roll(field_own[...], shift, 1).astype(jnp.bfloat16)
     dens_own[...] = shifted
     dens_slots[me] = shifted
-    to_everyone(lambda peer: dens_own, dens_slots, dens_sems)
+    def dens_out(step):
+        peer = partner if step == 1 else lax.rem(me + step, n)
+        return remote(dens_own, dens_slots.at[me], dens_sems.at[0, step], dens_sems.at[1, me], peer)
+
+    def dens_relay(step):
+        source = lax.rem(me + step, n)
+        return remote(
+            dens_slots.at[source], dens_slots.at[source], dens_sems.at[0, step + 1], dens_sems.at[1, source], partner
+        )
+
+    for step in (*range(2, n, 2), 1):
+        dens_out(step).start()
     for message in (1, 2):
         start_own(message)
 
     mine = jnp.clip(me - middle_first, 0, n // 2 - 1)
-    start = mine * own
-    left_col = pl.multiple_of(jnp.minimum(start // LANES * LANES, columns - 2 * LANES), LANES)
-    choose = (
-        lax.broadcasted_iota(jnp.int32, (own, 2 * LANES), 0) + (start - left_col)
-        == lax.broadcasted_iota(jnp.int32, (own, 2 * LANES), 1)
-    ).astype(jnp.bfloat16)
-    cols_own = dot(choose, walkers_ref[:, pl.ds(left_col, 2 * LANES)], CONTRACT_LAST).astype(jnp.bfloat16)
-    term[...] = cols_own
+    whole = mine // 2 * 3 + 2 * core_id
+    shared = mine // 2 * 3 + 1
+
+    def columns_of(walker):
+        return walkers_ref[:, pl.ds(pl.multiple_of(walker * occupied, occupied), occupied)]
+
+    def selector(count, offset):
+        return (
+            lax.broadcasted_iota(jnp.int32, (count, occupied), 0) + offset
+            == lax.broadcasted_iota(jnp.int32, (count, occupied), 1)
+        ).astype(jnp.bfloat16)
+
     out_line = lax.broadcasted_iota(jnp.int32, pick.shape, 0)
     out_row = lax.rem(out_line, height)
     wanted = jnp.where(out_row < own_rows, out_line // height * own_rows + out_row, -1)
@@ -343,94 +347,83 @@
             product = core_here * ahead_dot * back_dot
             sums[walker] += weight * jnp.sum(product.reshape(rows // 8, 8, window), axis=0)
 
-    owner = (start + lax.broadcasted_iota(jnp.int32, (own, 1), 0)) // occupied - start // occupied
-
     def take_fields():
         for step in range(1, n):
             peer = lax.rem(me + step, n)
             remote(
                 fields.at[pl.ds(0, span)], field_slots.at[peer], field_sems.at[0, 0], field_sems.at[1, peer], peer
             ).wait_recv()
-        chosen[...] = jnp.zeros_like(chosen)
-        for index in range(n):
-            there = pl.ds(index * rows // LANES * LANES, window)
-            for line in range(span):
-                chosen[line, :, there] += field_slots[index, line]
-
-    def add_chip(which):
-        where = near(which, 0) // 2
-        for side in range(2):
-            index = 2 * where + side
-            block = gathered[rows_of(index), :]
-            current = dot(term[...], block, CONTRACT_LAST).astype(jnp.bfloat16).astype(jnp.float32)
-            turn = lax.rem(window - lax.rem(index * rows, LANES), window)
-            lined = [pltpu.roll(field_slots[index, line], turn, 1)[:, :rows] for line in range(span)]
-            spread = lined[0]
-            for line in range(1, span):
-                spread = jnp.where(owner == line, lined[line], spread)
-            scaled = (spread * current).astype(jnp.bfloat16)
-            total[...] += dot(scaled, block, (((1,), (0,)), ((), ())))
+
+    def add_chip(chip_index):
+        here = pl.ds(pl.multiple_of(chip_index * 2 * rows, 16), 2 * rows)
+        block = gathered[here, :]
+        wide = (2 * rows + LANES - 1) // LANES * LANES
+        lined = []
+        for line in range(span):
+            row = jnp.zeros((1, wide), jnp.float32)
+            for side in range(2):
+                index = 2 * chip_index + side
+                part = jnp.concatenate(
+                    [field_slots[index, line], jnp.zeros((1, wide - window), jnp.float32)], axis=1
+                )
+                turn = lax.rem(side * rows - lax.rem(index * rows, LANES) + wide, wide)
+                row = row + pltpu.roll(part, turn, 1)
+            lined.append(row[:, : 2 * rows])
+        turned_map[...] = jnp.transpose(block)
+        whole_field = jnp.where(core_id == 0, lined[0], lined[1])
+        shared_field = jnp.where(core_id == 0, lined[1], lined[0])
+        plain = (((1,), (0,)), ((), ()))
+
+        def accumulate(target, scaled, firsts):
+            for first in firsts:
+                cols = slice(first, first + width)
+                stop = orbitals if first + width == main else first + width
+                target[:stop, cols] += dot(scaled[:stop], block[:, cols], plain)
+                if stop < orbitals:
+                    target[main:, cols] += dot(scaled[main:], block[:, cols], plain)
+
+        scaled = (turned_map[...].astype(jnp.float32) * whole_field).astype(jnp.bfloat16)
+        accumulate(gram, scaled, range(0, main, width))
+        gram[main:, main:] += dot(scaled[main:], block[:, main:], plain)
+        shared_map = (turned_map[...].astype(jnp.float32) * shared_field).astype(jnp.bfloat16)
+        shared_gram[main:, main:] += dot(shared_map[main:], block[:, main:], plain)
+
+        @pl.when(core_id == 0)
+        def _():
+            accumulate(shared_gram, shared_map, range(split, main, width))
+
+        @pl.when(core_id == 1)
+        def _():
+            accumulate(shared_gram, shared_map, range(0, split, width))
 
     corner_list = (
         me, partner, near(1, core_id), near(1, 1 - core_id), share(2), near(3, core_id), near(3, 1 - core_id),
-        near(4, core_id), near(4, 1 - core_id), near(7, core_id), near(7, 1 - core_id), share(5), share(6),
+        share(4), near(7, core_id), near(7, 1 - core_id), share(5), share(6),
     )
-    middle_list = {0: me, 1: partner, 3: share(1), 4: share(7), 7: share(6)}
-    stops = {1: (1, 0), 2: (1, 1), 4: (2, 0), 5: (2, 1), 8: (3, 0), 9: (3, 1)}
-    corner_stops = {11: (4, 0), 12: (4, 1)}
-    sides = {1: ((0,), ()), 3: ((1, 2), (7,)), 6: ((3, 4), (6,)), 10: ((5,), ())}
-    corner_sides = {10: (7,), 12: (6,)}
-    adds = {5: (0, 1), 6: (2, 7), 8: (3, 4, 6)}
+    middle_list = {0: me, 1: partner, 3: share(1), 4: share(7), 6: share(4), 7: share(6)}
+    stops = {1: (1, 0), 2: (1, 1), 4: (2, 0), 5: (2, 1)}
+    middle_far = {8: ((5, 0, False),), 9: ((5, 1, False),)}
+    corner_far = {
+        6: ((5, 0, True),), 7: ((7, 0, False),), 8: ((5, 1, True), (7, 1, False)),
+        11: ((6, 0, False), (6, 1, False)),
+    }
+    middle_sides = {1: (0,), 3: (1, 2, 7), 6: (3, 4, 6), 10: (5,)}
+    corner_sides = {1: (0,), 3: (1, 2), 6: (3,), 7: (4,), 9: (7,), 10: (5,), 11: (6,)}
+    add_order = (0, 1, 2, 7, 3, 4, 6, 5)
+    add_until = {4: 2, 5: 4, 7: 5, 8: 7, 10: 8}
 
     @pl.loop(0, len(corner_list))
     def _(task):
-        for number, (stage, chunk) in stops.items():
-
-            @pl.when(task == number)
-            def _():
-                point(stage, chunk)
-
-        for number, (stage, chunk) in corner_stops.items():
-
-            @pl.when(jnp.logical_and(task == number, is_corner))
-            def _():
-                point(stage, chunk)
-
-        for number, (both, middle) in sides.items():
-
-            @pl.when(task == number)
-            def _():
-                for which in both:
-                    land_side(which)
-
-                @pl.when(is_middle)
-                def _():
-                    for which in middle:
-                        land_side(which)
-
-        for number, those in corner_sides.items():
-
-            @pl.when(jnp.logical_and(task == number, is_corner))
-            def _():
-                for which in those:
-                    land_side(which)
-
-        pair = me
-        active = is_corner
-        for number, choice in enumerate(corner_list):
-            pair = jnp.where(task == number, choice, pair)
-        for number, choice in middle_list.items():
-            hit = jnp.logical_and(task == number, is_middle)
-            pair = jnp.where(hit, choice, pair)
-            active = jnp.logical_or(active, hit)
-
-        @pl.when(active)
+        @pl.when(task == 1)
         def _():
-            exchange(pair, jnp.where(task < 2, 1.0, 2.0))
-
-        @pl.when(task == 2)
-        def _():
-            from_everyone(lambda peer: dens_own, dens_slots, dens_sems)
+            for step in range(2, n, 2):
+                dens_relay(step).wait_recv()
+                dens_relay(step).start()
+            for step in range(0, n, 2):
+                source = lax.rem(partner + step, n)
+                remote(
+                    dens_own, dens_slots.at[source], dens_sems.at[0, 0], dens_sems.at[1, source], partner
+                ).wait_recv()
             dens_full[...] = jnp.zeros_like(dens_full)
             for index in range(n):
                 there = pl.ds(index * rows // LANES * LANES, window)
@@ -446,51 +439,113 @@
             for line in range(walker_count):
                 fields[line] = turned[line : line + 1]
             each_middle(lambda number, peer: field_send(number, peer).start())
-            field_slots[me] = fields[pl.ds(start // occupied, span)]
-
-        @pl.when(jnp.logical_and(task == 5, is_middle))
+            field_slots[me] = fields[pl.ds(mine * own // occupied, span)]
+
+        for number, (stage, chunk) in stops.items():
+
+            @pl.when(task == number)
+            def _():
+                point(stage, chunk)
+
+        for role, far_stops, side_stops in (
+            (is_middle, middle_far, middle_sides), (is_corner, corner_far, corner_sides)
+        ):
+            for number, those in far_stops.items():
+
+                @pl.when(jnp.logical_and(task == number, role))
+                def _():
+                    for which, chunk, onward in those:
+                        far_point(which, chunk, onward)
+
+            for number, those in side_stops.items():
+
+                @pl.when(jnp.logical_and(task == number, role))
+                def _():
+                    for which in those:
+                        land_side(which)
+
+        pair = me
+        active = is_corner
+        for number, choice in enumerate(corner_list):
+            pair = jnp.where(task == number, choice, pair)
+        for number, choice in middle_list.items():
+            hit = jnp.logical_and(task == number, is_middle)
+            pair = jnp.where(hit, choice, pair)
+            active = jnp.logical_or(active, hit)
+
+        @pl.when(active)
+        def _():
+            exchange(pair, jnp.where(task < 2, 1.0, 2.0))
+
+        @pl.when(jnp.logical_and(task == 4, is_middle))
         def _():
             take_fields()
 
-        for number, those in adds.items():
-
-            @pl.when(jnp.logical_and(task == number, is_middle))
-            def _():
-                for which in those:
-                    add_chip(which)
-
+        add_from, add_to = 0, 0
+        done = 0
+        for number, until in add_until.items():
+            add_from = jnp.where(task == number, done, add_from)
+            add_to = jnp.where(task == number, until, add_to)
+            done = until
+
+        @pl.loop(jnp.where(is_middle, add_from, 0), jnp.where(is_middle, add_to, 0))
+        def _(item):
+            place = me
+            for number, which in enumerate(add_order):
+                place = jnp.where(item == number, near(which, 0), place)
+            add_chip(place // 2)
 
     walker_exchange = jnp.sum(jnp.sum(sums[...], axis=1), axis=1, keepdims=True)
     energy_own[:walker_count, :] = (energy_own[:walker_count, :] - walker_exchange / occupied) / (2.0 * points)
     energy_slots[me] = energy_own[...]
     to_everyone(lambda peer: energy_own, energy_slots, energy_sems)
-    piece = next(p for p in (1280, 640, 256, points) if points % p == 0)
+    def gram_copy(side):
+        cols = slice(split, main) if side == 0 else slice(0, split)
+        return remote(
+            shared_half.at[:, cols], shared_half.at[:, cols], gram_sems.at[0], gram_sems.at[1], partner
+        )
+
+    def both_sides(act):
+        for side in range(2):
+
+            @pl.when(core_id == side)
+            def _():
+                act(side)
+
+    def apply(value, matrix):
+        parts = []
+        for first in range(0, main, width):
+            cols = slice(first, first + width)
+            part = dot(value[:, : first + width], matrix[: first + width, cols], (((1,), (0,)), ((), ())))
+            for later in range(first + width, main, width):
+                there = slice(later, later + width)
+                part = part + dot(value[:, there], matrix[cols, there], CONTRACT_LAST)
+            parts.append(part + dot(value[:, main:], matrix[main:, cols], (((1,), (0,)), ((), ()))))
+        last = dot(value[:, :main], matrix[main:, :main], CONTRACT_LAST)
+        parts.append(last + dot(value[:, main:], matrix[main:, main:], (((1,), (0,)), ((), ()))))
+        return jnp.concatenate(parts, axis=1)
 
     @pl.when(is_middle)
     def _():
-        add_chip(5)
-        running = term[...].astype(jnp.float32)
-        term[...] = total[...].astype(jnp.bfloat16)
-        running = running + term[...].astype(jnp.float32)
-        for degree in range(2, TAYLOR + 1):
-            total[...] = jnp.zeros_like(total)
-
-            @pl.loop(0, points // piece)
-            def _(number):
-                here = pl.ds(pl.multiple_of(number * piece, piece), piece)
-                block = gathered[here, :]
-                current = dot(term[...], block, CONTRACT_LAST).astype(jnp.bfloat16).astype(jnp.float32)
-                spread = chosen[0, :, here]
-                for line in range(1, span):
-                    spread = jnp.where(owner == line, chosen[line, :, here], spread)
-                scaled = (spread * current).astype(jnp.bfloat16)
-                total[...] += dot(scaled, block, (((1,), (0,)), ((), ())))
-
-            term[...] = (total[...] / degree).astype(jnp.bfloat16)
-            running = running + term[...].astype(jnp.float32)
-        final = running.astype(jnp.bfloat16)
-        first = dot(pick[...], final[:LANES], CONTRACT_LAST)
-        padded = jnp.concatenate([final[LANES:], jnp.zeros((half, orbitals), jnp.bfloat16)], axis=0)
+        def pack_shared(side):
+            cols = slice(split, main) if side == 0 else slice(0, split)
+            shared_half[:, cols] = shared_gram[:, cols].astype(jnp.bfloat16)
+            gram_copy(side).start()
+
+        both_sides(pack_shared)
+        shared_half[main:, main:] = shared_gram[main:, main:].astype(jnp.bfloat16)
+        whole_half[...] = gram[...].astype(jnp.bfloat16)
+        whole_term = dot(selector(occupied, 0), columns_of(whole), CONTRACT_LAST).astype(jnp.bfloat16)
+        shared_term = dot(selector(half, core_id * half), columns_of(shared), CONTRACT_LAST).astype(jnp.bfloat16)
+        whole_sum, shared_sum = whole_term.astype(jnp.float32), shared_term.astype(jnp.float32)
+        both_sides(lambda side: gram_copy(1 - side).wait_recv())
+        for degree in range(1, TAYLOR + 1):
+            whole_term = (apply(whole_term, whole_half) / degree).astype(jnp.bfloat16)
+            whole_sum = whole_sum + whole_term.astype(jnp.float32)
+            shared_term = (apply(shared_term, shared_half) / degree).astype(jnp.bfloat16)
+            shared_sum = shared_sum + shared_term.astype(jnp.float32)
+        first = dot(pick[...], whole_sum.astype(jnp.bfloat16), CONTRACT_LAST)
+        padded = jnp.concatenate([shared_sum, jnp.zeros((half, orbitals), jnp.float32)], axis=0).astype(jnp.bfloat16)
         second = dot(pick[...], padded, CONTRACT_LAST)
         for index in range(n):
             upper = second[index * height : index * height + height // 2]
@@ -513,20 +568,21 @@
         ).wait_recv()
     )
     out_lane = lax.broadcasted_iota(jnp.int32, (height, LANES), 1)
-    pieces = []
-    for number in range(n // 2):
-        got = incoming[number].astype(jnp.float32)
-        top_part, low_part = got[:height], got[height:]
-        pieces.append((top_part, 0))
-        pieces.append((top_part, 1))
-        pieces.append((jnp.concatenate([low_part, pltpu.roll(low_part, half, 1)], axis=0), 0))
-    for number in range(walker_count):
-        (low, low_at), (high, high_at) = pieces[2 * number], pieces[2 * number + 1]
-        low = pltpu.roll(low, half, 1) if low_at == 1 else low
-        high = pltpu.roll(high, half, 1) if high_at == 0 else high
-        out_ref[number] = jnp.where(out_lane < half, low, high)[:own_rows].astype(jnp.bfloat16)
-
-    all_sent(lambda peer: dens_own, dens_slots, dens_sems)
+    for number in range(0, n // 2, 2):
+        halves = []
+        for side in range(2):
+            got = incoming[number + side].astype(jnp.float32)
+            out_ref[number // 2 * 3 + 2 * side] = got[:own_rows].astype(jnp.bfloat16)
+            low_part = got[height:]
+            moved = pltpu.roll(low_part, half, 1)
+            halves.append(jnp.concatenate([moved, low_part] if side else [low_part, moved], axis=0))
+        joined = jnp.where(out_lane < half, halves[0], halves[1])
+        out_ref[number // 2 * 3 + 1] = joined[:own_rows].astype(jnp.bfloat16)
+
+    for step in (*range(2, n, 2), 1):
+        dens_out(step).wait_send()
+    for step in range(2, n, 2):
+        dens_relay(step).wait_send()
     all_sent(lambda peer: energy_own, energy_slots, energy_sems)
     each_middle(lambda number, peer: field_send(number, peer).wait_send())
 
@@ -538,12 +594,12 @@
         sent(in_sems, number, range(3), inner)
     for number in range(3):
         sent(out_sems_map, number, range(3), outer)
-    for number in range(7):
+    for number in range(8):
         sent(side_sems, number, range(3), partner)
-    sent(side_sems, 7, range(3), partner)
 
     @pl.when(is_middle)
     def _():
+        both_sides(lambda side: gram_copy(side).wait_send())
         sent(in_sems, 2, (0,), inner)
         sent(across_sems, 0, range(3), across)
         sent(across_sems, 1, range(3), across)
@@ -575,7 +631,7 @@
     dma = pltpu.SemaphoreType.DMA
     vmem = pltpu.VMEM
     return pl.pallas_call(
-        functools.partial(fused_kernel, n, walker_count),
+        functools.partial(fused_kernel, n, walker_count, own),
         out_shape=(
             jax.ShapeDtypeStruct((walker_count, own_rows, occupied), jnp.bfloat16),
             jax.ShapeDtypeStruct((lines, LANES), jnp.float32),
@@ -591,15 +647,17 @@
             vmem((rows, columns), jnp.bfloat16),
             vmem((window, columns), jnp.bfloat16),
             vmem((walker_count, 8, window), jnp.float32),
-            vmem((own, orbitals), jnp.float32),
-            vmem((own, orbitals), jnp.bfloat16),
+            vmem((orbitals, 2 * rows), jnp.bfloat16),
+            vmem((orbitals, orbitals), jnp.float32),
+            vmem((orbitals, orbitals), jnp.float32),
+            vmem((orbitals, orbitals), jnp.bfloat16),
+            vmem((orbitals, orbitals), jnp.bfloat16),
             vmem((lines, window), jnp.bfloat16),
             vmem((n, lines, window), jnp.bfloat16),
             vmem((lines, full), jnp.float32),
             vmem((lines, window), jnp.float32),
             vmem((n, span, 1, window), jnp.float32),
             vmem((lines, 1, window), jnp.float32),
-            vmem((span, 1, full), jnp.float32),
             vmem((lines, LANES), jnp.float32),
             vmem((n, lines, LANES), jnp.float32),
             vmem((n * height, orbitals), jnp.bfloat16),
@@ -615,6 +673,7 @@
             dma((2, n)),
             dma((2, n)),
             dma((2, n)),
+            dma((2,)),
         ],
         compiler_params=pltpu.CompilerParams(
             collective_id=0, has_side_effects=True, vmem_limit_bytes=60 * 2**20
@@ -706,7 +765,7 @@
     own_rows = orbitals // n
     own_cols = walker_count * occupied // n
     rest = orbitals % LANES
-    if point_rows % 16 == 0 and n == 16 and 4 * own_cols == 3 * LANES and occupied == LANES and rest and LANES % rest == 0:
+    if point_rows % 16 == 0 and n == 16 and 4 * own_cols == 3 * LANES and orbitals // LANES % 2 == 0 and occupied == LANES and rest and LANES % rest == 0:
         placed, energy = fused(n, points_map, trial, core, jnp.moveaxis(walkers, 1, 0), draws.T)
         return jnp.moveaxis(placed, 0, 1), energy[:walker_count, 0]
     flat_walkers = walkers.reshape(orbitals, walker_count * occupied)

time: 90.5 us -> 87.4 us (0.966)
  Pallas kernels: 86.7 us -> 83.6 us
    pallas_call x1, Pallas kernels: 86.7 us -> 83.6 us  [fused(): pl.pallas_call(functools.partial(fused_kernel, n, walker_count, own), out...]
where the time goes in v4:
time: 87.4 us; the launch traced here: 87.2 us
  Pallas kernels  83.6 us (96%)
  local copies, waits for them, and re-layouts  2.92 us (3%)
    pallas_call x1, Pallas kernels, fused(): pl.pallas_call(functools.partial(fused_kernel, n, walker_count, own), out...  83.6 us

profile of v4, /device:TPU:0, one launch (start us, length us, event | category | flops | bytes accessed | tf_op | source)
XLA Modules:
  0.0 87.2 jit_solution(12671999848160931461)
XLA Ops:
  0.6 83.6 %fused.1 = (bf16[12,50,128]{2,1,0:T(8,128)(2,1)}, f32[16,128]{1,0:T(8,128)}) custom-call(bf16[400,800]{1,0:T(8,128)(2,1)} %map_hbm.1, bf16[6400,128]{1,0:T(8,128)(2,1)} %trial_hbm.1, bf16[400,6400]{1,0:T(8,128)(2,1)} %core_hbm.1, bf16[12,800,128]{2,1,0:T(8,128)(2,1)} %bitcast.3, s32[12,400]{1,0:T(8,128)} %bitcast.5), custom_call_target="tpu_custom_call" | custom-call | tf_op jit(solution)/shard_map/fused/pallas_call | solution.py:633
  84.3 1.3 %slice_reduce_fusion = f32[12]{0:T(128)} fusion(f32[16,128]{1,0:T(8,128)} %get-tuple-element.5), kind=kLoop, calls=%fused_computation | loop fusion | bytes 96 | tf_op jit(solution)/shard_map/slice | solution.py:770
  85.6 1.6 %copy.8 = bf16[50,12,128]{2,0,1:T(8,128)(2,1)} copy(bf16[50,12,128]{2,0,1:T(8,128)(2,1)} %bitcast.4) | data formatting | bytes 307200
